TPU v7x, 32 devices: a whole 2x2x4 slice. The times are simulated.
32 devices in a mesh: layer: 8 (over y, x, core), dp: 4 (over z).
Axes of the slice: x: 2, y: 2, z: 4, core: 2. Of those that a mesh axis runs over, the one named last changes fastest.
Arguments:
- weights: bfloat16 [32, 512, 512], P('layer', 'dp'), may hold values from -0.25 to 0.25
- biases: float32 [32, 512], P('layer'), may hold values from -3 to 3
- guesses: float32 [8, 2048, 512], P('layer', 'dp'), may hold values from -6 to 6
Outputs:
- states: bfloat16 [32, 2048, 512], P('layer', 'dp')
All inputs are finite; a program needn't handle non-finite values.
Results may differ from a plain program's by a relative error of at most 0.0041.
Values may be sent and summed in bfloat16 or wider, within the bound.
No kernel may reach another device: no remote copies, remote signals or barrier semaphores. Data moves between devices by JAX's collectives and lax.ppermute only.
A program may use at most 64 MiB of HBM per device.

v0:
```python
import functools

import jax
import jax.numpy as jnp
from jax import lax
from jax.experimental import pallas as pl
from jax.experimental.pallas import tpu as pltpu
from jax.sharding import PartitionSpec as P


GROUP = 4
BIAS_ROWS = 16
PIECE_MASKS = (0, 2, 1, 3)
BF16 = jnp.bfloat16
F32 = jnp.float32
VMEM = pl.BlockSpec(memory_space=pltpu.VMEM)
SMEM = pl.BlockSpec(memory_space=pltpu.SMEM)


def call(kernel, out_shapes, in_specs, args, flops, scratch=(), limit=16 * 2**20, out_specs=None):
    nbytes = sum(a.size * a.dtype.itemsize for a in args)
    return pl.pallas_call(
        kernel,
        out_shape=out_shapes,
        in_specs=in_specs,
        out_specs=jax.tree.map(lambda _: VMEM, out_shapes) if out_specs is None else out_specs,
        scratch_shapes=list(scratch),
        compiler_params=pltpu.CompilerParams(vmem_limit_bytes=limit),
        cost_estimate=pl.CostEstimate(flops=flops, bytes_accessed=nbytes, transcendentals=0),
    )(*args)


def gather_pieces(piece, axis):
    if lax.axis_size(axis) != 4:
        return [lax.all_gather(piece, axis, axis=piece.ndim - 2, tiled=True)]
    across = lax.ppermute(piece, axis, [(0, 2), (2, 0), (1, 3), (3, 1)])
    beside = lax.ppermute(piece, axis, [(0, 1), (1, 0), (2, 3), (3, 2)])
    middle = lax.ppermute(piece, axis, [(1, 2), (2, 1)])
    passed = lax.ppermute(across, axis, [(1, 0), (2, 3)])
    return [piece, across, beside, middle, passed]


def put_pieces(own_ref, pieces, target, lead):
    rows = pieces[0].shape[-2]
    if len(pieces) == 1:
        target[(*lead, pl.ds(0, rows))] = pieces[0][...]
        return
    for number, mask in enumerate(PIECE_MASKS):
        at = pl.multiple_of((own_ref[1] ^ mask) * rows, rows)
        value = pieces[number][...]
        if number == 3 and len(pieces) == 5:
            value = value + pieces[4][...]
        target[(*lead, pl.ds(at, rows))] = value


def cut_kernel(weight_ref, bias_in_ref, head_ref, rest_ref, bias_ref, flight):
    copies = [
        pltpu.make_async_copy(weight_ref.at[0], head_ref, flight.at[0]),
        pltpu.make_async_copy(weight_ref.at[pl.ds(1, rest_ref.shape[0])], rest_ref, flight.at[1]),
        pltpu.make_async_copy(bias_in_ref, bias_ref, flight.at[2]),
    ]
    for copy in copies:
        copy.start()
    for copy in copies:
        copy.wait()


def head_kernel(own_ref, bias_ref, *refs):
    *pieces, out_ref = refs
    width = out_ref.shape[1]
    put_pieces(own_ref, pieces, out_ref, ())
    bias = bias_ref[0:1, :]
    high = bias.astype(BF16)
    rest = bias - high.astype(F32)
    mid = rest.astype(BF16)
    low = (rest - mid.astype(F32)).astype(BF16)
    row = lax.broadcasted_iota(jnp.int32, (BIAS_ROWS, width), 0)
    tail = jnp.where(row == 0, high, jnp.where(row == 1, mid, jnp.where(row == 2, low, jnp.zeros_like(low))))
    out_ref[pl.ds(width, BIAS_ROWS), :] = tail.astype(BF16)


def turn_of(state, weight, bias):
    return jnp.tanh(jnp.dot(state.astype(BF16), weight, preferred_element_type=F32) + bias)


def fine_kernel(fine_width, count, own_ref, bias_ref, guess_ref, head_ref, *refs):
    depth = bias_ref.shape[0]
    rows, width = guess_ref.shape
    pieces, tau_refs, rest_ref = refs[: -count - 1], refs[-count - 1 : -1], refs[-1]
    rank = own_ref[0]
    part_rows = rows // count
    half = count // 2
    states, totals = [], [None, None]
    for part in range(2):
        states.append(
            jnp.concatenate(
                [
                    guess_ref[pl.ds(pl.multiple_of((rank ^ mask) * part_rows, part_rows), part_rows), :]
                    for mask in range(part * half, (part + 1) * half)
                ],
                axis=0,
            )
        )
    for layer_no in range(depth):
        if layer_no == 0:
            weight = head_ref[pl.ds(0, width), :]
        else:
            put_pieces(own_ref, [p.at[layer_no - 1] for p in pieces], rest_ref, (layer_no - 1,))
            weight = rest_ref[layer_no - 1]
        bias = bias_ref[layer_no : layer_no + 1, :]
        for part in range(2):
            turn = turn_of(states[part], weight, bias)
            totals[part] = (1.0 - depth) * turn if layer_no == 0 else totals[part] + turn
            if layer_no < depth - 1:
                states[part] = states[part] + fine_width * turn
    for part in range(2):
        tau = (fine_width * totals[part]).astype(BF16)
        for number in range(half):
            tau_refs[part * half + number][...] = tau[number * part_rows : (number + 1) * part_rows]


def last_kernel(fine_width, own_ref, bias_ref, guess_ref, head_ref, rest_ref, *refs):
    *corrected_refs, out_ref, stage, flight = refs
    depth = bias_ref.shape[0]
    rows, width = guess_ref.shape
    count = len(corrected_refs)
    rank = own_ref[0]
    part_rows = rows // count
    half = count // 2
    places = [pl.multiple_of((rank ^ mask) * part_rows, part_rows) for mask in range(count)]
    states, bases, copies = [], [], []
    for part in range(2):
        masks = range(part * half, (part + 1) * half)
        states.append(
            jnp.concatenate(
                [
                    jnp.where(
                        rank == 0,
                        guess_ref[pl.ds(places[mask], part_rows), :],
                        corrected_refs[mask][...].astype(F32),
                    )
                    for mask in masks
                ],
                axis=0,
            )
        )
        bases.append(pl.multiple_of(((rank // half) ^ part) * (rows // 2), rows // 2))
    for layer_no in range(depth):
        weight = head_ref[pl.ds(0, width), :] if layer_no == 0 else rest_ref[layer_no - 1]
        bias = bias_ref[layer_no : layer_no + 1, :]
        for part in range(2):
            states[part] = states[part] + fine_width * turn_of(states[part], weight, bias)
            rounded = states[part].astype(BF16)
            for number in range(half):
                stage[layer_no, pl.ds(places[part * half + number], part_rows), :] = rounded[
                    number * part_rows : (number + 1) * part_rows
                ]
            block = pl.ds(bases[part], rows // 2)
            copy = pltpu.make_async_copy(
                stage.at[layer_no, block], out_ref.at[layer_no, block], flight.at[2 * layer_no + part]
            )
            copy.start()
            copies.append(copy)
    for copy in copies:
        copy.wait()


def hold_kernel(masks, own_ref, *refs):
    *heads, held_ref, flight = refs
    rank = own_ref[0]
    copies = [
        pltpu.make_async_copy(head, held_ref.at[rank ^ jnp.where(rank % 2 == 0, *masks[number])], flight.at[number])
        for number, head in enumerate(heads)
    ]
    for copy in copies:
        copy.start()
    for copy in copies:
        copy.wait()


def split_kernel(own_ref, guess_ref, *out_refs):
    part_rows = out_refs[0].shape[0]
    for mask, out_ref in enumerate(out_refs):
        out_ref[...] = guess_ref[pl.ds(pl.multiple_of((own_ref[0] ^ mask) * part_rows, part_rows), part_rows), :]


def coarse_kernel(block_width, own_ref, held_ref, *refs):
    *refs, tau, guess, found = refs
    count, rows, width = guess.shape
    guess_refs, tau_refs, out_refs = refs[:count], refs[count : 2 * count], refs[2 * count :]
    rank = own_ref[0]
    for mask in range(count):
        guess[rank ^ mask] = guess_refs[mask][...]
        tau[rank ^ mask] = tau_refs[mask][...]
    phase = lax.broadcasted_iota(jnp.int32, (rows, width), 0) % GROUP

    def step(block, carry):
        level, corrected, jump = carry
        before = block - 1
        both = jnp.concatenate([level, corrected], axis=0)
        tail = held_ref[before, pl.ds(width, BIAS_ROWS), :].astype(F32)
        bias = (tail[0:1, :] + tail[1:2, :]) + tail[2:3, :]
        turn = turn_of(both, held_ref[before, pl.ds(0, width), :], bias)
        turn_level, turn_corrected = turn[:rows], turn[rows:]
        jump = jnp.where(
            phase == before % GROUP,
            (corrected - level) + (GROUP * block_width) * (turn_corrected - turn_level),
            jump,
        )
        here = tau[before].astype(F32)
        arrival = level + block_width * turn_level + here
        moved = corrected + block_width * turn_corrected + here
        own = phase == block % GROUP
        level = jnp.where(own, guess[block], arrival)
        corrected = jnp.where(own, arrival + jump, moved)
        found[block] = corrected.astype(BF16)
        return level, corrected, jump

    first = guess[0]
    found[0] = first.astype(BF16)
    carry = (first, first, jnp.zeros_like(first))
    if count <= 8:
        for block in range(1, count):
            carry = step(block, carry)
    else:
        lax.fori_loop(1, count, step, carry)
    for mask in range(count):
        out_refs[mask][...] = found[rank ^ mask]


def gather_heads(head):
    count = lax.axis_size("layer")
    chip_bits = [1 << k for k in range(1, count.bit_length() - 1)]
    orders = (chip_bits, chip_bits[::-1])
    held, masks = [head], [(0, 0)]
    for turn_no in range(len(chip_bits)):
        bits = (orders[0][turn_no], orders[1][turn_no])
        pairs = [(source, source ^ bits[source & 1]) for source in range(count)]
        held = held + [lax.ppermute(value, "layer", pairs) for value in held]
        masks = masks + [(even ^ bits[0], odd ^ bits[1]) for even, odd in masks]
    pairs = [(source, source ^ 1) for source in range(count)]
    held = held + [lax.ppermute(value, "layer", pairs) for value in held]
    masks = masks + [(odd ^ 1, even ^ 1) for even, odd in masks]
    return held, masks


def exchange(values):
    count = len(values)
    return [values[0]] + [
        lax.ppermute(values[mask], "layer", [(source, source ^ mask) for source in range(count)])
        for mask in range(1, count)
    ]


def per_device(weights, biases, guesses):
    count = lax.axis_size("layer")
    own = jnp.stack([lax.axis_index("layer"), lax.axis_index("dp")]).astype(jnp.int32)
    depth, _, width = weights.shape
    rows = guesses.shape[1]
    fine_width = 4.0 / (depth * count)
    block_width = depth * fine_width
    initial = guesses[0]
    part_rows = rows // count
    part = jax.ShapeDtypeStruct((part_rows, width), BF16)

    head_own, rest_own, biases = call(
        cut_kernel,
        (
            jax.ShapeDtypeStruct(weights.shape[1:], BF16),
            jax.ShapeDtypeStruct((depth - 1, *weights.shape[1:]), BF16),
            jax.ShapeDtypeStruct(biases.shape, F32),
        ),
        [pl.BlockSpec(memory_space=pltpu.HBM)] * 2,
        (weights, biases),
        1 << 20,
        (pltpu.SemaphoreType.DMA((3,)),),
    )
    head_pieces = gather_pieces(head_own, "dp")
    rest_pieces = gather_pieces(rest_own, "dp")
    guess_parts = call(
        split_kernel,
        (jax.ShapeDtypeStruct((part_rows, width), F32),) * count,
        [SMEM, VMEM],
        (own, initial),
        1 << 20,
    )
    guess_parts = exchange(guess_parts)
    head = call(
        head_kernel,
        jax.ShapeDtypeStruct((width + BIAS_ROWS, width), BF16),
        [SMEM] + [VMEM] * (1 + len(head_pieces)),
        (own, biases, *head_pieces),
        1 << 20,
    )
    heads, masks = gather_heads(head)

    *tau, rest = call(
        functools.partial(fine_kernel, fine_width, count),
        (part,) * count + (jax.ShapeDtypeStruct((depth - 1, width, width), BF16),),
        [SMEM] + [VMEM] * (3 + len(rest_pieces)),
        (own, biases, initial, head, *rest_pieces),
        2 * depth * rows * width * width,
    )
    tau = exchange(tau)
    held_size = 2 * count * (width + BIAS_ROWS) * width
    held = call(
        functools.partial(hold_kernel, masks),
        jax.ShapeDtypeStruct((count, width + BIAS_ROWS, width), BF16),
        [SMEM] + [pl.BlockSpec(memory_space=pl.ANY)] * count,
        (own, *heads),
        1 << 28,
        (pltpu.SemaphoreType.DMA((count,)),),
        limit=held_size + 2 * 2**20,
    )
    corrected = call(
        functools.partial(coarse_kernel, block_width),
        (part,) * count,
        [SMEM] + [VMEM] * (1 + 2 * count),
        (own, held, *guess_parts, *tau),
        4 * rows * width * width,
        tuple(pltpu.VMEM((count, part_rows, width), kind) for kind in (BF16, F32, BF16)),
        limit=held_size + 12 * 2**20,
    )
    corrected = exchange(corrected)
    return call(
        functools.partial(last_kernel, fine_width),
        jax.ShapeDtypeStruct((depth, rows, width), BF16),
        [SMEM] + [VMEM] * (4 + count),
        (own, biases, initial, head, rest, *corrected),
        2 * depth * rows * width * width,
        (pltpu.VMEM((depth, rows, width), BF16), pltpu.SemaphoreType.DMA((2 * depth,))),
        out_specs=pl.BlockSpec(memory_space=pl.ANY),
    )


def solution(mesh):
    in_specs = (P("layer", "dp", None), P("layer", None), P("layer", "dp", None))
    out_specs = P("layer", "dp", None)

    return jax.shard_map(per_device, mesh=mesh, in_specs=in_specs, out_specs=out_specs, check_vma=False)
```

profile of v0, /device:TPU:0, one launch (start us, length us, event | category | flops | bytes accessed | tf_op | source)
XLA Modules:
  0.0 112.4 jit_solution(1648429280886356925)
XLA Ops:
  2.1 4.1 %collective-permute-start = (bf16[128,512]{1,0:T(8,128)(2,1)S(1)}, bf16[128,512]{1,0:T(8,128)(2,1)S(1)}, u32[]{:S(2)}, u32[]{:S(2)}) collective-permute-start(bf16[128,512]{1,0:T(8,128)(2,1)S(1)} %get-tuple-element.34.refs_0_), channel_id=1, source_target_pairs={{0,2},{2,0},{1,3},{3,1},{4,6},{6,4},{5,7},{7,5},{8,10},{10,8},{9,1... | collective-permute-start | bytes 393224 | tf_op jit(solution)/shard_map/ppermute | solution.py:36
  6.3 1.6 %collective-permute-start.1 = (bf16[128,512]{1,0:T(8,128)(2,1)S(1)}, bf16[128,512]{1,0:T(8,128)(2,1)S(1)}, u32[]{:S(2)}, u32[]{:S(2)}) collective-permute-start(bf16[128,512]{1,0:T(8,128)(2,1)S(1)} %get-tuple-element.34.refs_0_), channel_id=1, source_target_pairs={{0,1},{1,0},{2,3},{3,2},{4,5},{5,4},{6,7},{7,6},{8,9},{9,8},{10,11... | collective-permute-start | bytes 393224 | tf_op jit(solution)/shard_map/ppermute | solution.py:37
  8.5 4.9 %collective-permute-done.refs_1_ = bf16[128,512]{1,0:T(8,128)(2,1)S(1)} collective-permute-done((bf16[128,512]{1,0:T(8,128)(2,1)S(1)}, bf16[128,512]{1,0:T(8,128)(2,1)S(1)}, u32[]{:S(2)}, u32[]{:S(2)}) %collective-permute-start) | collective-permute-done | bytes 131104 | tf_op jit(solution)/shard_map/ppermute | solution.py:36
  14.8 5.5 %collective-permute-done.3.refs_4_ = bf16[128,512]{1,0:T(8,128)(2,1)S(1)} collective-permute-done((bf16[128,512]{1,0:T(8,128)(2,1)S(1)}, bf16[128,512]{1,0:T(8,128)(2,1)S(1)}, u32[]{:S(2)}, u32[]{:S(2)}) %collective-permute-start.3) | collective-permute-done | bytes 131104 | tf_op jit(solution)/shard_map/ppermute | solution.py:39
  20.9 1.7 %collective-permute-start.8 = (bf16[528,512]{1,0:T(8,128)(2,1)S(1)}, bf16[528,512]{1,0:T(8,128)(2,1)S(1)}, u32[]{:S(2)}, u32[]{:S(2)}) collective-permute-start(bf16[528,512]{1,0:T(8,128)(2,1)S(1)} %shard_map.38.head_ref.refs_0_), channel_id=1, source_target_pairs={{0,8},{4,20},{8,0},{12,28},{16,24},{20,4},{24,16},{28,12},{1,9},{5... | collective-permute-start | bytes 1622024 | tf_op jit(solution)/shard_map/ppermute | solution.py:239
  23.7 1.3 %collective-permute-start.17 = (f32[64,512]{1,0:T(8,128)S(1)}, f32[64,512]{1,0:T(8,128)S(1)}, u32[]{:S(2)}, u32[]{:S(2)}) collective-permute-start(f32[64,512]{1,0:T(8,128)S(1)} %get-tuple-element.40), channel_id=1, source_target_pairs={{0,12},{4,8},{8,4},{12,0},{16,28},{20,24},{24,20},{28,16},{1,13},{... | collective-permute-start | bytes 393224 | tf_op jit(solution)/shard_map/ppermute | solution.py:250
  25.1 1.5 %collective-permute-start.18 = (f32[64,512]{1,0:T(8,128)S(1)}, f32[64,512]{1,0:T(8,128)S(1)}, u32[]{:S(2)}, u32[]{:S(2)}) collective-permute-start(f32[64,512]{1,0:T(8,128)S(1)} %get-tuple-element.41), channel_id=1, source_target_pairs={{0,16},{4,20},{8,24},{12,28},{16,0},{20,4},{24,8},{28,12},{1,17},{... | collective-permute-start | bytes 393224 | tf_op jit(solution)/shard_map/ppermute | solution.py:250
  26.8 10.5 %collective-permute-done.16.refs_2_ = f32[64,512]{1,0:T(8,128)S(1)} collective-permute-done((f32[64,512]{1,0:T(8,128)S(1)}, f32[64,512]{1,0:T(8,128)S(1)}, u32[]{:S(2)}, u32[]{:S(2)}) %collective-permute-start.16) | collective-permute-done | bytes 131104 | tf_op jit(solution)/shard_map/ppermute | solution.py:250
  37.3 1.5 %collective-permute-start.9 = (bf16[528,512]{1,0:T(8,128)(2,1)S(1)}, bf16[528,512]{1,0:T(8,128)(2,1)S(1)}, u32[]{:S(2)}, u32[]{:S(2)}) collective-permute-start(bf16[528,512]{1,0:T(8,128)(2,1)S(1)} %shard_map.38.head_ref.refs_0_), channel_id=1, source_target_pairs={{0,16},{4,12},{8,24},{12,4},{16,0},{20,28},{24,8},{28,20},{1,17},{... | collective-permute-start | bytes 1622024 | tf_op jit(solution)/shard_map/ppermute | solution.py:239
  40.1 2.6 %collective-permute-start.20 = (f32[64,512]{1,0:T(8,128)S(1)}, f32[64,512]{1,0:T(8,128)S(1)}, u32[]{:S(2)}, u32[]{:S(2)}) collective-permute-start(f32[64,512]{1,0:T(8,128)S(1)} %get-tuple-element.43), channel_id=1, source_target_pairs={{0,24},{4,28},{8,16},{12,20},{16,8},{20,12},{24,0},{28,4},{1,25},{... | collective-permute-start | bytes 393224 | tf_op jit(solution)/shard_map/ppermute | solution.py:250
  43.8 2.5 %collective-permute-start.5 = (bf16[3,128,512]{2,1,0:T(8,128)(2,1)S(1)}, bf16[3,128,512]{2,1,0:T(8,128)(2,1)S(1)}, u32[]{:S(2)}, u32[]{:S(2)}) collective-permute-start(bf16[3,128,512]{2,1,0:T(8,128)(2,1)S(1)} %get-tuple-element.35.refs_0_), channel_id=1, source_target_pairs={{0,1},{1,0},{2,3},{3,2},{4,5},{5,4},{6,7},{7,6},{8,9},{9,8},{10,11... | collective-permute-start | bytes 1179656 | tf_op jit(solution)/shard_map/ppermute | solution.py:37
  48.1 15.8 %collective-permute-done.4.refs_1_ = bf16[3,128,512]{2,1,0:T(8,128)(2,1)S(1)} collective-permute-done((bf16[3,128,512]{2,1,0:T(8,128)(2,1)S(1)}, bf16[3,128,512]{2,1,0:T(8,128)(2,1)S(1)}, u32[]{:S(2)}, u32[]{:S(2)}) %collective-permute-start.4) | collective-permute-done | bytes 393248 | tf_op jit(solution)/shard_map/ppermute | solution.py:36
  66.3 11.0 %collective-permute-done.7.refs_4_ = bf16[3,128,512]{2,1,0:T(8,128)(2,1)S(1)} collective-permute-done((bf16[3,128,512]{2,1,0:T(8,128)(2,1)S(1)}, bf16[3,128,512]{2,1,0:T(8,128)(2,1)S(1)}, u32[]{:S(2)}, u32[]{:S(2)}) %collective-permute-start.7) | collective-permute-done | bytes 393248 | tf_op jit(solution)/shard_map/ppermute | solution.py:39
  77.3 2.2 %shard_map.39 = (bf16[64,512]{1,0:T(8,128)(2,1)S(1)}, bf16[64,512]{1,0:T(8,128)(2,1)S(1)}, bf16[64,512]{1,0:T(8,128)(2,1)S(1)}, bf16[64,512]{1,0:T(8,128)(2,1)S(...) custom-call(s32[2]{0:T(128)S(1)} %pad_add_fusion.own_ref, ...), custom_call_target="tpu_custom_call" | custom-call | flops 1073741824 | bytes 3563528 | tf_op jit(solution)/shard_map/pallas_call | solution.py:22
  79.6 4.3 %collective-permute-done.21.refs_7_ = f32[64,512]{1,0:T(8,128)S(1)} collective-permute-done((f32[64,512]{1,0:T(8,128)S(1)}, f32[64,512]{1,0:T(8,128)S(1)}, u32[]{:S(2)}, u32[]{:S(2)}) %collective-permute-start.21) | collective-permute-done | bytes 131104 | tf_op jit(solution)/shard_map/ppermute | solution.py:250
  85.7 2.9 %collective-permute-done.23.refs_10_ = bf16[64,512]{1,0:T(8,128)(2,1)S(1)} collective-permute-done((bf16[64,512]{1,0:T(8,128)(2,1)S(1)}, bf16[64,512]{1,0:T(8,128)(2,1)S(1)}, u32[]{:S(2)}, u32[]{:S(2)}) %collective-permute-start.23) | collective-permute-done | bytes 65568 | tf_op jit(solution)/shard_map/ppermute | solution.py:250
  90.2 2.8 %collective-permute-start.28 = (bf16[64,512]{1,0:T(8,128)(2,1)S(1)}, bf16[64,512]{1,0:T(8,128)(2,1)S(1)}, u32[]{:S(2)}, u32[]{:S(2)}) collective-permute-start(bf16[64,512]{1,0:T(8,128)(2,1)S(1)} %get-tuple-element.52), channel_id=1, source_target_pairs={{0,28},{4,24},{8,20},{12,16},{16,12},{20,8},{24,4},{28,0},{1,29},{... | collective-permute-start | bytes 196616 | tf_op jit(solution)/shard_map/ppermute | solution.py:250
  94.9 1.8 %collective-permute-done.28.refs_15_ = bf16[64,512]{1,0:T(8,128)(2,1)S(1)} collective-permute-done((bf16[64,512]{1,0:T(8,128)(2,1)S(1)}, bf16[64,512]{1,0:T(8,128)(2,1)S(1)}, u32[]{:S(2)}, u32[]{:S(2)}) %collective-permute-start.28) | collective-permute-done | bytes 65568 | tf_op jit(solution)/shard_map/ppermute | solution.py:250
  96.7 2.4 %shard_map.42 = (bf16[64,512]{1,0:T(8,128)(2,1)S(1)}, bf16[64,512]{1,0:T(8,128)(2,1)S(1)}, bf16[64,512]{1,0:T(8,128)(2,1)S(1)}, bf16[64,512]{1,0:T(8,128)(2,1)S(...) custom-call(s32[2]{0:T(128)S(1)} %pad_add_fusion.own_ref, ...), custom_call_target="tpu_custom_call" | custom-call | flops 536870912 | bytes 5898248 | tf_op jit(solution)/shard_map/pallas_call | solution.py:22
  99.8 1.3 %collective-permute-start.31 = (bf16[64,512]{1,0:T(8,128)(2,1)S(1)}, bf16[64,512]{1,0:T(8,128)(2,1)S(1)}, u32[]{:S(2)}, u32[]{:S(2)}) collective-permute-start(bf16[64,512]{1,0:T(8,128)(2,1)S(1)} %get-tuple-element.56), channel_id=1, source_target_pairs={{0,12},{4,8},{8,4},{12,0},{16,28},{20,24},{24,20},{28,16},{1,13},{... | collective-permute-start | bytes 196616 | tf_op jit(solution)/shard_map/ppermute | solution.py:250
  101.5 1.3 %collective-permute-start.33 = (bf16[64,512]{1,0:T(8,128)(2,1)S(1)}, bf16[64,512]{1,0:T(8,128)(2,1)S(1)}, u32[]{:S(2)}, u32[]{:S(2)}) collective-permute-start(bf16[64,512]{1,0:T(8,128)(2,1)S(1)} %get-tuple-element.58), channel_id=1, source_target_pairs={{0,20},{4,16},{8,28},{12,24},{16,4},{20,0},{24,12},{28,8},{1,21},{... | collective-permute-start | bytes 196616 | tf_op jit(solution)/shard_map/ppermute | solution.py:250
  106.0 1.8 %collective-permute-done.33.refs_5_ = bf16[64,512]{1,0:T(8,128)(2,1)S(1)} collective-permute-done((bf16[64,512]{1,0:T(8,128)(2,1)S(1)}, bf16[64,512]{1,0:T(8,128)(2,1)S(1)}, u32[]{:S(2)}, u32[]{:S(2)}) %collective-permute-start.33) | collective-permute-done | bytes 65568 | tf_op jit(solution)/shard_map/ppermute | solution.py:250
  108.2 1.4 %collective-permute-done.35.refs_7_ = bf16[64,512]{1,0:T(8,128)(2,1)S(1)} collective-permute-done((bf16[64,512]{1,0:T(8,128)(2,1)S(1)}, bf16[64,512]{1,0:T(8,128)(2,1)S(1)}, u32[]{:S(2)}, u32[]{:S(2)}) %collective-permute-start.35) | collective-permute-done | bytes 65568 | tf_op jit(solution)/shard_map/ppermute | solution.py:250
  109.6 2.8 %shard_map.43 = bf16[4,512,512]{2,1,0:T(8,128)(2,1)} custom-call(s32[2]{0:T(128)S(1)} %pad_add_fusion.own_ref, f32[4,512]{1,0:T(4,128)S(1)} %get-tuple-element.33.bias_ref, f32[512,512]{1,0:T(8,128)S(1)} %bitcast.5, bf16[528,512]{1,0:T(8,128)(2,1)S(1)} %shard_map.38.head_ref.refs_0_, bf16[3,512,512]{2,1,0:T(8,128)(2,1)S(1)} %get-tuple-element.36.rest_ref, ...), custom_call_target="tpu_custom_call" | custom-call | flops 1073741824 | bytes 3694600 | tf_op jit(solution)/shard_map/pallas_call | solution.py:22
  (62 shorter events, 22.6 us)
Async XLA Ops:
  2.1 11.3 %collective-permute-start = (bf16[128,512]{1,0:T(8,128)(2,1)S(1)}, bf16[128,512]{1,0:T(8,128)(2,1)S(1)}, u32[]{:S(2)}, u32[]{:S(2)}) collective-permute-start(bf16[128,512]{1,0:T(8,128)(2,1)S(1)} %get-tuple-element.34.refs_0_), channel_id=1, source_target_pairs={{0,2},{2,0},{1,3},{3,1},{4,6},{6,4},{5,7},{7,5},{8,10},{10,8},{9,1... | collective-permute-start | bytes 393224 | tf_op jit(solution)/shard_map/ppermute | solution.py:36
  6.3 8.5 %collective-permute-start.1 = (bf16[128,512]{1,0:T(8,128)(2,1)S(1)}, bf16[128,512]{1,0:T(8,128)(2,1)S(1)}, u32[]{:S(2)}, u32[]{:S(2)}) collective-permute-start(bf16[128,512]{1,0:T(8,128)(2,1)S(1)} %get-tuple-element.34.refs_0_), channel_id=1, source_target_pairs={{0,1},{1,0},{2,3},{3,2},{4,5},{5,4},{6,7},{7,6},{8,9},{9,8},{10,11... | collective-permute-start | bytes 393224 | tf_op jit(solution)/shard_map/ppermute | solution.py:37
  7.8 7.0 %collective-permute-start.2 = (bf16[128,512]{1,0:T(8,128)(2,1)S(1)}, bf16[128,512]{1,0:T(8,128)(2,1)S(1)}, u32[]{:S(2)}, u32[]{:S(2)}) collective-permute-start(bf16[128,512]{1,0:T(8,128)(2,1)S(1)} %get-tuple-element.34.refs_0_), channel_id=1, source_target_pairs={{1,2},{2,1},{5,6},{6,5},{9,10},{10,9},{13,14},{14,13},{17,18},{18,... | collective-permute-start | bytes 393224 | tf_op jit(solution)/shard_map/ppermute | solution.py:38
  13.4 6.8 %collective-permute-start.3 = (bf16[128,512]{1,0:T(8,128)(2,1)S(1)}, bf16[128,512]{1,0:T(8,128)(2,1)S(1)}, u32[]{:S(2)}, u32[]{:S(2)}) collective-permute-start(bf16[128,512]{1,0:T(8,128)(2,1)S(1)} %collective-permute-done.refs_1_), channel_id=1, source_target_pairs={{1,0},{2,3},{5,4},{6,7},{9,8},{10,11},{13,12},{14,15},{17,16},{18,... | collective-permute-start | bytes 393224 | tf_op jit(solution)/shard_map/ppermute | solution.py:39
  20.9 17.9 %collective-permute-start.8 = (bf16[528,512]{1,0:T(8,128)(2,1)S(1)}, bf16[528,512]{1,0:T(8,128)(2,1)S(1)}, u32[]{:S(2)}, u32[]{:S(2)}) collective-permute-start(bf16[528,512]{1,0:T(8,128)(2,1)S(1)} %shard_map.38.head_ref.refs_0_), channel_id=1, source_target_pairs={{0,8},{4,20},{8,0},{12,28},{16,24},{20,4},{24,16},{28,12},{1,9},{5... | collective-permute-start | bytes 1622024 | tf_op jit(solution)/shard_map/ppermute | solution.py:239
  23.2 14.1 %collective-permute-start.16 = (f32[64,512]{1,0:T(8,128)S(1)}, f32[64,512]{1,0:T(8,128)S(1)}, u32[]{:S(2)}, u32[]{:S(2)}) collective-permute-start(f32[64,512]{1,0:T(8,128)S(1)} %get-tuple-element.39), channel_id=1, source_target_pairs={{0,8},{4,12},{8,0},{12,4},{16,24},{20,28},{24,16},{28,20},{1,9},{5... | collective-permute-start | bytes 393224 | tf_op jit(solution)/shard_map/ppermute | solution.py:250
  23.7 16.4 %collective-permute-start.17 = (f32[64,512]{1,0:T(8,128)S(1)}, f32[64,512]{1,0:T(8,128)S(1)}, u32[]{:S(2)}, u32[]{:S(2)}) collective-permute-start(f32[64,512]{1,0:T(8,128)S(1)} %get-tuple-element.40), channel_id=1, source_target_pairs={{0,12},{4,8},{8,4},{12,0},{16,28},{20,24},{24,20},{28,16},{1,13},{... | collective-permute-start | bytes 393224 | tf_op jit(solution)/shard_map/ppermute | solution.py:250
  25.1 17.6 %collective-permute-start.18 = (f32[64,512]{1,0:T(8,128)S(1)}, f32[64,512]{1,0:T(8,128)S(1)}, u32[]{:S(2)}, u32[]{:S(2)}) collective-permute-start(f32[64,512]{1,0:T(8,128)S(1)} %get-tuple-element.41), channel_id=1, source_target_pairs={{0,16},{4,20},{8,24},{12,28},{16,0},{20,4},{24,8},{28,12},{1,17},{... | collective-permute-start | bytes 393224 | tf_op jit(solution)/shard_map/ppermute | solution.py:250
  26.6 17.2 %collective-permute-start.19 = (f32[64,512]{1,0:T(8,128)S(1)}, f32[64,512]{1,0:T(8,128)S(1)}, u32[]{:S(2)}, u32[]{:S(2)}) collective-permute-start(f32[64,512]{1,0:T(8,128)S(1)} %get-tuple-element.42), channel_id=1, source_target_pairs={{0,20},{4,16},{8,28},{12,24},{16,4},{20,0},{24,12},{28,8},{1,21},{... | collective-permute-start | bytes 393224 | tf_op jit(solution)/shard_map/ppermute | solution.py:250
  37.3 28.5 %collective-permute-start.9 = (bf16[528,512]{1,0:T(8,128)(2,1)S(1)}, bf16[528,512]{1,0:T(8,128)(2,1)S(1)}, u32[]{:S(2)}, u32[]{:S(2)}) collective-permute-start(bf16[528,512]{1,0:T(8,128)(2,1)S(1)} %shard_map.38.head_ref.refs_0_), channel_id=1, source_target_pairs={{0,16},{4,12},{8,24},{12,4},{16,0},{20,28},{24,8},{28,20},{1,17},{... | collective-permute-start | bytes 1622024 | tf_op jit(solution)/shard_map/ppermute | solution.py:239
  38.8 27.1 %collective-permute-start.10 = (bf16[528,512]{1,0:T(8,128)(2,1)S(1)}, bf16[528,512]{1,0:T(8,128)(2,1)S(1)}, u32[]{:S(2)}, u32[]{:S(2)}) collective-permute-start(bf16[528,512]{1,0:T(8,128)(2,1)S(1)} %collective-permute-done.8.refs_1_), channel_id=1, source_target_pairs={{0,16},{4,12},{8,24},{12,4},{16,0},{20,28},{24,8},{28,20},{1,17},{... | collective-permute-start | bytes 1622024 | tf_op jit(solution)/shard_map/ppermute | solution.py:239
  40.1 7.3 %collective-permute-start.20 = (f32[64,512]{1,0:T(8,128)S(1)}, f32[64,512]{1,0:T(8,128)S(1)}, u32[]{:S(2)}, u32[]{:S(2)}) collective-permute-start(f32[64,512]{1,0:T(8,128)S(1)} %get-tuple-element.43), channel_id=1, source_target_pairs={{0,24},{4,28},{8,16},{12,20},{16,8},{20,12},{24,0},{28,4},{1,25},{... | collective-permute-start | bytes 393224 | tf_op jit(solution)/shard_map/ppermute | solution.py:250
  42.7 21.2 %collective-permute-start.4 = (bf16[3,128,512]{2,1,0:T(8,128)(2,1)S(1)}, bf16[3,128,512]{2,1,0:T(8,128)(2,1)S(1)}, u32[]{:S(2)}, u32[]{:S(2)}) collective-permute-start(bf16[3,128,512]{2,1,0:T(8,128)(2,1)S(1)} %get-tuple-element.35.refs_0_), channel_id=1, source_target_pairs={{0,2},{2,0},{1,3},{3,1},{4,6},{6,4},{5,7},{7,5},{8,10},{10,8},{9,1... | collective-permute-start | bytes 1179656 | tf_op jit(solution)/shard_map/ppermute | solution.py:36
  43.8 20.1 %collective-permute-start.5 = (bf16[3,128,512]{2,1,0:T(8,128)(2,1)S(1)}, bf16[3,128,512]{2,1,0:T(8,128)(2,1)S(1)}, u32[]{:S(2)}, u32[]{:S(2)}) collective-permute-start(bf16[3,128,512]{2,1,0:T(8,128)(2,1)S(1)} %get-tuple-element.35.refs_0_), channel_id=1, source_target_pairs={{0,1},{1,0},{2,3},{3,2},{4,5},{5,4},{6,7},{7,6},{8,9},{9,8},{10,11... | collective-permute-start | bytes 1179656 | tf_op jit(solution)/shard_map/ppermute | solution.py:37
  47.4 17.8 %collective-permute-start.6 = (bf16[3,128,512]{2,1,0:T(8,128)(2,1)S(1)}, bf16[3,128,512]{2,1,0:T(8,128)(2,1)S(1)}, u32[]{:S(2)}, u32[]{:S(2)}) collective-permute-start(bf16[3,128,512]{2,1,0:T(8,128)(2,1)S(1)} %get-tuple-element.35.refs_0_), channel_id=1, source_target_pairs={{1,2},{2,1},{5,6},{6,5},{9,10},{10,9},{13,14},{14,13},{17,18},{18,... | collective-permute-start | bytes 1179656 | tf_op jit(solution)/shard_map/ppermute | solution.py:38
  63.9 19.9 %collective-permute-start.11 = (bf16[528,512]{1,0:T(8,128)(2,1)S(1)}, bf16[528,512]{1,0:T(8,128)(2,1)S(1)}, u32[]{:S(2)}, u32[]{:S(2)}) collective-permute-start(bf16[528,512]{1,0:T(8,128)(2,1)S(1)} %shard_map.38.head_ref.refs_0_), channel_id=1, source_target_pairs={{0,4},{4,0},{8,12},{12,8},{16,20},{20,16},{24,28},{28,24},{1,5},{5... | collective-permute-start | bytes 1622024 | tf_op jit(solution)/shard_map/ppermute | solution.py:242
  63.9 13.4 %collective-permute-start.7 = (bf16[3,128,512]{2,1,0:T(8,128)(2,1)S(1)}, bf16[3,128,512]{2,1,0:T(8,128)(2,1)S(1)}, u32[]{:S(2)}, u32[]{:S(2)}) collective-permute-start(bf16[3,128,512]{2,1,0:T(8,128)(2,1)S(1)} %collective-permute-done.4.refs_1_), channel_id=1, source_target_pairs={{1,0},{2,3},{5,4},{6,7},{9,8},{10,11},{13,12},{14,15},{17,16},{18,... | collective-permute-start | bytes 1179656 | tf_op jit(solution)/shard_map/ppermute | solution.py:39
  65.2 23.9 %collective-permute-start.12 = (bf16[528,512]{1,0:T(8,128)(2,1)S(1)}, bf16[528,512]{1,0:T(8,128)(2,1)S(1)}, u32[]{:S(2)}, u32[]{:S(2)}) collective-permute-start(bf16[528,512]{1,0:T(8,128)(2,1)S(1)} %collective-permute-done.8.refs_1_), channel_id=1, source_target_pairs={{0,4},{4,0},{8,12},{12,8},{16,20},{20,16},{24,28},{28,24},{1,5},{5... | collective-permute-start | bytes 1622024 | tf_op jit(solution)/shard_map/ppermute | solution.py:242
  65.8 23.6 %collective-permute-start.13 = (bf16[528,512]{1,0:T(8,128)(2,1)S(1)}, bf16[528,512]{1,0:T(8,128)(2,1)S(1)}, u32[]{:S(2)}, u32[]{:S(2)}) collective-permute-start(bf16[528,512]{1,0:T(8,128)(2,1)S(1)} %collective-permute-done.9.refs_2_), channel_id=1, source_target_pairs={{0,4},{4,0},{8,12},{12,8},{16,20},{20,16},{24,28},{28,24},{1,5},{5... | collective-permute-start | bytes 1622024 | tf_op jit(solution)/shard_map/ppermute | solution.py:242
  65.9 24.3 %collective-permute-start.14 = (bf16[528,512]{1,0:T(8,128)(2,1)S(1)}, bf16[528,512]{1,0:T(8,128)(2,1)S(1)}, u32[]{:S(2)}, u32[]{:S(2)}) collective-permute-start(bf16[528,512]{1,0:T(8,128)(2,1)S(1)} %collective-permute-done.10.refs_3_), channel_id=1, source_target_pairs={{0,4},{4,0},{8,12},{12,8},{16,20},{20,16},{24,28},{28,24},{1,5},{5... | collective-permute-start | bytes 1622024 | tf_op jit(solution)/shard_map/ppermute | solution.py:242
  77.3 6.5 %collective-permute-start.21 = (f32[64,512]{1,0:T(8,128)S(1)}, f32[64,512]{1,0:T(8,128)S(1)}, u32[]{:S(2)}, u32[]{:S(2)}) collective-permute-start(f32[64,512]{1,0:T(8,128)S(1)} %get-tuple-element.44), channel_id=1, source_target_pairs={{0,28},{4,24},{8,20},{12,16},{16,12},{20,8},{24,4},{28,0},{1,29},{... | collective-permute-start | bytes 393224 | tf_op jit(solution)/shard_map/ppermute | solution.py:250
  85.1 9.0 %collective-permute-start.24 = (bf16[64,512]{1,0:T(8,128)(2,1)S(1)}, bf16[64,512]{1,0:T(8,128)(2,1)S(1)}, u32[]{:S(2)}, u32[]{:S(2)}) collective-permute-start(bf16[64,512]{1,0:T(8,128)(2,1)S(1)} %get-tuple-element.48), channel_id=1, source_target_pairs={{0,12},{4,8},{8,4},{12,0},{16,28},{20,24},{24,20},{28,16},{1,13},{... | collective-permute-start | bytes 196616 | tf_op jit(solution)/shard_map/ppermute | solution.py:250
  90.2 6.6 %collective-permute-start.28 = (bf16[64,512]{1,0:T(8,128)(2,1)S(1)}, bf16[64,512]{1,0:T(8,128)(2,1)S(1)}, u32[]{:S(2)}, u32[]{:S(2)}) collective-permute-start(bf16[64,512]{1,0:T(8,128)(2,1)S(1)} %get-tuple-element.52), channel_id=1, source_target_pairs={{0,28},{4,24},{8,20},{12,16},{16,12},{20,8},{24,4},{28,0},{1,29},{... | collective-permute-start | bytes 196616 | tf_op jit(solution)/shard_map/ppermute | solution.py:250
  101.5 6.3 %collective-permute-start.33 = (bf16[64,512]{1,0:T(8,128)(2,1)S(1)}, bf16[64,512]{1,0:T(8,128)(2,1)S(1)}, u32[]{:S(2)}, u32[]{:S(2)}) collective-permute-start(bf16[64,512]{1,0:T(8,128)(2,1)S(1)} %get-tuple-element.58), channel_id=1, source_target_pairs={{0,20},{4,16},{8,28},{12,24},{16,4},{20,0},{24,12},{28,8},{1,21},{... | collective-permute-start | bytes 196616 | tf_op jit(solution)/shard_map/ppermute | solution.py:250
  (15 other events, 78.1 us)
where the time goes:
time: 113 us; the launch traced here: 112 us
  waiting for transfers between devices  65.2 us (58%)
  starting transfers between devices  35.2 us (31%)
  Pallas kernels  10.1 us (9%)
  local copies, waits for them, and re-layouts  1.74 us (2%)
    ppermute x21, waiting for transfers between devices, exchange(): lax.ppermute(values[mask], 'layer', [(source, source ^ mask) for source i...  27.9 us
    ppermute x2, waiting for transfers between devices, gather_pieces(): across = lax.ppermute(piece, axis, [(0, 2), (2, 0), (1, 3), (3, 1)])  20.7 us
    ppermute x21, starting transfers between devices, exchange(): lax.ppermute(values[mask], 'layer', [(source, source ^ mask) for source i...  17.2 us
    ppermute x2, waiting for transfers between devices, gather_pieces(): passed = lax.ppermute(across, axis, [(1, 0), (2, 3)])  16.5 us
    pallas_call x7, Pallas kernels, call(): pl.pallas_call(kernel, out_shape=out_shapes, in_specs=in_specs, out_specs...  10.1 us
    ppermute x2, starting transfers between devices, gather_pieces(): across = lax.ppermute(piece, axis, [(0, 2), (2, 0), (1, 3), (3, 1)])  5.25 us
    ppermute x7, starting transfers between devices, gather_heads(): held = held + [lax.ppermute(value, 'layer', pairs) for value in held]  4.77 us
    ppermute x2, starting transfers between devices, gather_pieces(): beside = lax.ppermute(piece, axis, [(0, 1), (1, 0), (2, 3), (3, 2)])  4.06 us
  transfers between devices with their start and end apart: 36, of which 17 were waited for; matrix products, arithmetic and copies ran while one was open for 0% of the time, Pallas kernels for 4%

commit v1 on v0

--- a/solution.py
+++ b/solution.py
@@ -30,9 +30,21 @@
     )(*args)
 
 
-def gather_pieces(piece, axis):
+def gather_whole(piece, axis):
+    return [lax.all_gather(piece, axis, axis=piece.ndim - 2, tiled=True)]
+
+
+def gather_direct(piece, axis):
     if lax.axis_size(axis) != 4:
-        return [lax.all_gather(piece, axis, axis=piece.ndim - 2, tiled=True)]
+        return gather_whole(piece, axis)
+    return [piece] + [
+        lax.ppermute(piece, axis, [(source, source ^ mask) for source in range(4)]) for mask in PIECE_MASKS[1:]
+    ]
+
+
+def gather_passed(piece, axis):
+    if lax.axis_size(axis) != 4:
+        return gather_whole(piece, axis)
     across = lax.ppermute(piece, axis, [(0, 2), (2, 0), (1, 3), (3, 1)])
     beside = lax.ppermute(piece, axis, [(0, 1), (1, 0), (2, 3), (3, 2)])
     middle = lax.ppermute(piece, axis, [(1, 2), (2, 1)])
@@ -51,18 +63,6 @@
         if number == 3 and len(pieces) == 5:
             value = value + pieces[4][...]
         target[(*lead, pl.ds(at, rows))] = value
-
-
-def cut_kernel(weight_ref, bias_in_ref, head_ref, rest_ref, bias_ref, flight):
-    copies = [
-        pltpu.make_async_copy(weight_ref.at[0], head_ref, flight.at[0]),
-        pltpu.make_async_copy(weight_ref.at[pl.ds(1, rest_ref.shape[0])], rest_ref, flight.at[1]),
-        pltpu.make_async_copy(bias_in_ref, bias_ref, flight.at[2]),
-    ]
-    for copy in copies:
-        copy.start()
-    for copy in copies:
-        copy.wait()
 
 
 def head_kernel(own_ref, bias_ref, *refs):
@@ -263,20 +263,8 @@
     part_rows = rows // count
     part = jax.ShapeDtypeStruct((part_rows, width), BF16)
 
-    head_own, rest_own, biases = call(
-        cut_kernel,
-        (
-            jax.ShapeDtypeStruct(weights.shape[1:], BF16),
-            jax.ShapeDtypeStruct((depth - 1, *weights.shape[1:]), BF16),
-            jax.ShapeDtypeStruct(biases.shape, F32),
-        ),
-        [pl.BlockSpec(memory_space=pltpu.HBM)] * 2,
-        (weights, biases),
-        1 << 20,
-        (pltpu.SemaphoreType.DMA((3,)),),
-    )
-    head_pieces = gather_pieces(head_own, "dp")
-    rest_pieces = gather_pieces(rest_own, "dp")
+    head_pieces = gather_direct(weights[0], "dp")
+    rest_pieces = gather_passed(weights[1:], "dp")
     guess_parts = call(
         split_kernel,
         (jax.ShapeDtypeStruct((part_rows, width), F32),) * count,

time: 113 us -> 109 us (0.965)
  waiting for transfers between devices: 65.2 us -> 60.1 us
  local copies, waits for them, and re-layouts: 1.74 us -> 3.95 us
    ppermute x21, waiting for transfers between devices: 27.9 us -> 22.4 us  [exchange(): lax.ppermute(values[mask], 'layer', [(source, source ^ mask) for source i...]
    ppermute x8 -> x7, starting transfers between devices: 13.2 us -> 12 us  [the longest x3 5.71 us: gather_direct(): lax.ppermute(piece, axis, [(source, source ^ mask) for source in range(4)])]
    ppermute x8 -> x7, waiting for transfers between devices: 37.2 us -> 37.7 us  [the longest x1 17.6 us: gather_passed(): across = lax.ppermute(piece, axis, [(0, 2), (2, 0), (1, 3), (3, 1)])]
    pallas_call x7 -> x6, Pallas kernels: 10.1 us -> 9.72 us  [call(): pl.pallas_call(kernel, out_shape=out_shapes, in_specs=in_specs, out_specs...]
  transfers between devices with their start and end apart: 36 -> 35, of which waited for: 17 -> 16; matrix products, arithmetic and copies ran while one was open for 0% -> 1% of each run, Pallas kernels for 4% -> 4%
where the time goes in v1:
time: 109 us; the launch traced here: 108 us
  waiting for transfers between devices  60.1 us (55%)
  starting transfers between devices  34.2 us (31%)
  Pallas kernels  9.72 us (9%)
  local copies, waits for them, and re-layouts  3.95 us (4%)
    ppermute x21, waiting for transfers between devices, exchange(): lax.ppermute(values[mask], 'layer', [(source, source ^ mask) for source i...  22.4 us
    ppermute x21, starting transfers between devices, exchange(): lax.ppermute(values[mask], 'layer', [(source, source ^ mask) for source i...  18 us
    ppermute x1, waiting for transfers between devices, gather_passed(): across = lax.ppermute(piece, axis, [(0, 2), (2, 0), (1, 3), (3, 1)])  17.6 us
    ppermute x1, waiting for transfers between devices, gather_passed(): passed = lax.ppermute(across, axis, [(1, 0), (2, 3)])  10.5 us
    pallas_call x6, Pallas kernels, call(): pl.pallas_call(kernel, out_shape=out_shapes, in_specs=in_specs, out_specs...  9.72 us
    ppermute x3, waiting for transfers between devices, gather_direct(): lax.ppermute(piece, axis, [(source, source ^ mask) for source in range(4)])  8.66 us
    ppermute x3, starting transfers between devices, gather_direct(): lax.ppermute(piece, axis, [(source, source ^ mask) for source in range(4)])  5.71 us
    ppermute x1, starting transfers between devices, gather_passed(): across = lax.ppermute(piece, axis, [(0, 2), (2, 0), (1, 3), (3, 1)])  4.31 us
  transfers between devices with their start and end apart: 35, of which 16 were waited for; matrix products, arithmetic and copies ran while one was open for 1% of the time, Pallas kernels for 4%

profile of v1, /device:TPU:0, one launch (start us, length us, event | category | flops | bytes accessed | tf_op | source)
XLA Modules:
  0.0 108.3 jit_solution(1633943347001412477)
XLA Ops:
  1.0 4.1 %collective-permute-start = (bf16[128,512]{1,0:T(8,128)(2,1)S(1)}, bf16[128,512]{1,0:T(8,128)(2,1)S(1)}, u32[]{:S(2)}, u32[]{:S(2)}) collective-permute-start(bf16[128,512]{1,0:T(8,128)(2,1)S(1)} %slice_bitcast_fusion.refs_0_), channel_id=1, source_target_pairs={{0,2},{1,3},{2,0},{3,1},{4,6},{5,7},{6,4},{7,5},{8,10},{9,11},{10,... | collective-permute-start | bytes 393224 | tf_op jit(solution)/shard_map/ppermute | solution.py:41
  5.1 1.6 %collective-permute-start.1 = (bf16[128,512]{1,0:T(8,128)(2,1)S(1)}, bf16[128,512]{1,0:T(8,128)(2,1)S(1)}, u32[]{:S(2)}, u32[]{:S(2)}) collective-permute-start(bf16[128,512]{1,0:T(8,128)(2,1)S(1)} %slice_bitcast_fusion.refs_0_), channel_id=1, source_target_pairs={{0,1},{1,0},{2,3},{3,2},{4,5},{5,4},{6,7},{7,6},{8,9},{9,8},{10,11... | collective-permute-start | bytes 393224 | tf_op jit(solution)/shard_map/ppermute | solution.py:41
  6.8 6.3 %collective-permute-done.refs_1_ = bf16[128,512]{1,0:T(8,128)(2,1)S(1)} collective-permute-done((bf16[128,512]{1,0:T(8,128)(2,1)S(1)}, bf16[128,512]{1,0:T(8,128)(2,1)S(1)}, u32[]{:S(2)}, u32[]{:S(2)}) %collective-permute-start) | collective-permute-done | bytes 131104 | tf_op jit(solution)/shard_map/ppermute | solution.py:41
  13.1 2.3 %collective-permute-done.2.refs_3_ = bf16[128,512]{1,0:T(8,128)(2,1)S(1)} collective-permute-done((bf16[128,512]{1,0:T(8,128)(2,1)S(1)}, bf16[128,512]{1,0:T(8,128)(2,1)S(1)}, u32[]{:S(2)}, u32[]{:S(2)}) %collective-permute-start.2) | collective-permute-done | bytes 131104 | tf_op jit(solution)/shard_map/ppermute | solution.py:41
  16.8 1.6 %collective-permute-start.7 = (bf16[528,512]{1,0:T(8,128)(2,1)S(1)}, bf16[528,512]{1,0:T(8,128)(2,1)S(1)}, u32[]{:S(2)}, u32[]{:S(2)}) collective-permute-start(bf16[528,512]{1,0:T(8,128)(2,1)S(1)} %shard_map.37.head_ref.refs_0_), channel_id=1, source_target_pairs={{0,8},{4,20},{8,0},{12,28},{16,24},{20,4},{24,16},{28,12},{1,9},{5... | collective-permute-start | bytes 1622024 | tf_op jit(solution)/shard_map/ppermute | solution.py:239
  22.1 1.5 %collective-permute-start.17 = (f32[64,512]{1,0:T(8,128)S(1)}, f32[64,512]{1,0:T(8,128)S(1)}, u32[]{:S(2)}, u32[]{:S(2)}) collective-permute-start(f32[64,512]{1,0:T(8,128)S(1)} %get-tuple-element.35), channel_id=1, source_target_pairs={{0,16},{4,20},{8,24},{12,28},{16,0},{20,4},{24,8},{28,12},{1,17},{... | collective-permute-start | bytes 393224 | tf_op jit(solution)/shard_map/ppermute | solution.py:250
  23.8 8.0 %collective-permute-done.15.refs_2_ = f32[64,512]{1,0:T(8,128)S(1)} collective-permute-done((f32[64,512]{1,0:T(8,128)S(1)}, f32[64,512]{1,0:T(8,128)S(1)}, u32[]{:S(2)}, u32[]{:S(2)}) %collective-permute-start.15) | collective-permute-done | bytes 131104 | tf_op jit(solution)/shard_map/ppermute | solution.py:250
  31.8 1.5 %collective-permute-start.8 = (bf16[528,512]{1,0:T(8,128)(2,1)S(1)}, bf16[528,512]{1,0:T(8,128)(2,1)S(1)}, u32[]{:S(2)}, u32[]{:S(2)}) collective-permute-start(bf16[528,512]{1,0:T(8,128)(2,1)S(1)} %shard_map.37.head_ref.refs_0_), channel_id=1, source_target_pairs={{0,16},{4,12},{8,24},{12,4},{16,0},{20,28},{24,8},{28,20},{1,17},{... | collective-permute-start | bytes 1622024 | tf_op jit(solution)/shard_map/ppermute | solution.py:239
  34.6 2.7 %collective-permute-start.19 = (f32[64,512]{1,0:T(8,128)S(1)}, f32[64,512]{1,0:T(8,128)S(1)}, u32[]{:S(2)}, u32[]{:S(2)}) collective-permute-start(f32[64,512]{1,0:T(8,128)S(1)} %get-tuple-element.37), channel_id=1, source_target_pairs={{0,24},{4,28},{8,16},{12,20},{16,8},{20,12},{24,0},{28,4},{1,25},{... | collective-permute-start | bytes 393224 | tf_op jit(solution)/shard_map/ppermute | solution.py:250
  38.3 4.3 %collective-permute-start.3 = (bf16[3,128,512]{2,1,0:T(8,128)(2,1)S(1)}, bf16[3,128,512]{2,1,0:T(8,128)(2,1)S(1)}, u32[]{:S(2)}, u32[]{:S(2)}) collective-permute-start(bf16[3,128,512]{2,1,0:T(8,128)(2,1)S(1)} %slice.7.refs_0_), channel_id=1, source_target_pairs={{0,2},{2,0},{1,3},{3,1},{4,6},{6,4},{5,7},{7,5},{8,10},{10,8},{9,1... | collective-permute-start | bytes 1179656 | tf_op jit(solution)/shard_map/ppermute | solution.py:48
  43.3 17.6 %collective-permute-done.3.refs_1_ = bf16[3,128,512]{2,1,0:T(8,128)(2,1)S(1)} collective-permute-done((bf16[3,128,512]{2,1,0:T(8,128)(2,1)S(1)}, bf16[3,128,512]{2,1,0:T(8,128)(2,1)S(1)}, u32[]{:S(2)}, u32[]{:S(2)}) %collective-permute-start.3) | collective-permute-done | bytes 393248 | tf_op jit(solution)/shard_map/ppermute | solution.py:48
  61.8 1.3 %collective-permute-start.6 = (bf16[3,128,512]{2,1,0:T(8,128)(2,1)S(1)}, bf16[3,128,512]{2,1,0:T(8,128)(2,1)S(1)}, u32[]{:S(2)}, u32[]{:S(2)}) collective-permute-start(bf16[3,128,512]{2,1,0:T(8,128)(2,1)S(1)} %collective-permute-done.3.refs_1_), channel_id=1, source_target_pairs={{1,0},{2,3},{5,4},{6,7},{9,8},{10,11},{13,12},{14,15},{17,16},{18,... | collective-permute-start | bytes 1179656 | tf_op jit(solution)/shard_map/ppermute | solution.py:51
  63.8 10.5 %collective-permute-done.6.refs_4_ = bf16[3,128,512]{2,1,0:T(8,128)(2,1)S(1)} collective-permute-done((bf16[3,128,512]{2,1,0:T(8,128)(2,1)S(1)}, bf16[3,128,512]{2,1,0:T(8,128)(2,1)S(1)}, u32[]{:S(2)}, u32[]{:S(2)}) %collective-permute-start.6) | collective-permute-done | bytes 393248 | tf_op jit(solution)/shard_map/ppermute | solution.py:51
  74.4 2.2 %shard_map.38 = (bf16[64,512]{1,0:T(8,128)(2,1)S(1)}, bf16[64,512]{1,0:T(8,128)(2,1)S(1)}, bf16[64,512]{1,0:T(8,128)(2,1)S(1)}, bf16[64,512]{1,0:T(8,128)(2,1)S(...) custom-call(s32[2]{0:T(128)S(1)} %pad_add_fusion.own_ref, ...), custom_call_target="tpu_custom_call" | custom-call | flops 1073741824 | bytes 3563528 | tf_op jit(solution)/shard_map/pallas_call | solution.py:22
  76.6 3.4 %collective-permute-done.20.refs_7_ = f32[64,512]{1,0:T(8,128)S(1)} collective-permute-done((f32[64,512]{1,0:T(8,128)S(1)}, f32[64,512]{1,0:T(8,128)S(1)}, u32[]{:S(2)}, u32[]{:S(2)}) %collective-permute-start.20) | collective-permute-done | bytes 131104 | tf_op jit(solution)/shard_map/ppermute | solution.py:250
  81.9 2.9 %collective-permute-done.22.refs_10_ = bf16[64,512]{1,0:T(8,128)(2,1)S(1)} collective-permute-done((bf16[64,512]{1,0:T(8,128)(2,1)S(1)}, bf16[64,512]{1,0:T(8,128)(2,1)S(1)}, u32[]{:S(2)}, u32[]{:S(2)}) %collective-permute-start.22) | collective-permute-done | bytes 65568 | tf_op jit(solution)/shard_map/ppermute | solution.py:250
  86.4 2.7 %collective-permute-start.27 = (bf16[64,512]{1,0:T(8,128)(2,1)S(1)}, bf16[64,512]{1,0:T(8,128)(2,1)S(1)}, u32[]{:S(2)}, u32[]{:S(2)}) collective-permute-start(bf16[64,512]{1,0:T(8,128)(2,1)S(1)} %get-tuple-element.46), channel_id=1, source_target_pairs={{0,28},{4,24},{8,20},{12,16},{16,12},{20,8},{24,4},{28,0},{1,29},{... | collective-permute-start | bytes 196616 | tf_op jit(solution)/shard_map/ppermute | solution.py:250
  90.9 1.7 %collective-permute-done.27.refs_15_ = bf16[64,512]{1,0:T(8,128)(2,1)S(1)} collective-permute-done((bf16[64,512]{1,0:T(8,128)(2,1)S(1)}, bf16[64,512]{1,0:T(8,128)(2,1)S(1)}, u32[]{:S(2)}, u32[]{:S(2)}) %collective-permute-start.27) | collective-permute-done | bytes 65568 | tf_op jit(solution)/shard_map/ppermute | solution.py:250
  92.6 2.4 %shard_map.41 = (bf16[64,512]{1,0:T(8,128)(2,1)S(1)}, bf16[64,512]{1,0:T(8,128)(2,1)S(1)}, bf16[64,512]{1,0:T(8,128)(2,1)S(1)}, bf16[64,512]{1,0:T(8,128)(2,1)S(...) custom-call(s32[2]{0:T(128)S(1)} %pad_add_fusion.own_ref, ...), custom_call_target="tpu_custom_call" | custom-call | flops 536870912 | bytes 5898248 | tf_op jit(solution)/shard_map/pallas_call | solution.py:22
  97.3 1.4 %collective-permute-start.32 = (bf16[64,512]{1,0:T(8,128)(2,1)S(1)}, bf16[64,512]{1,0:T(8,128)(2,1)S(1)}, u32[]{:S(2)}, u32[]{:S(2)}) collective-permute-start(bf16[64,512]{1,0:T(8,128)(2,1)S(1)} %get-tuple-element.52), channel_id=1, source_target_pairs={{0,20},{4,16},{8,28},{12,24},{16,4},{20,0},{24,12},{28,8},{1,21},{... | collective-permute-start | bytes 196616 | tf_op jit(solution)/shard_map/ppermute | solution.py:250
  98.7 1.4 %collective-permute-start.33 = (bf16[64,512]{1,0:T(8,128)(2,1)S(1)}, bf16[64,512]{1,0:T(8,128)(2,1)S(1)}, u32[]{:S(2)}, u32[]{:S(2)}) collective-permute-start(bf16[64,512]{1,0:T(8,128)(2,1)S(1)} %get-tuple-element.53), channel_id=1, source_target_pairs={{0,24},{4,28},{8,16},{12,20},{16,8},{20,12},{24,0},{28,4},{1,25},{... | collective-permute-start | bytes 196616 | tf_op jit(solution)/shard_map/ppermute | solution.py:250
  102.3 1.8 %collective-permute-done.33.refs_6_ = bf16[64,512]{1,0:T(8,128)(2,1)S(1)} collective-permute-done((bf16[64,512]{1,0:T(8,128)(2,1)S(1)}, bf16[64,512]{1,0:T(8,128)(2,1)S(1)}, u32[]{:S(2)}, u32[]{:S(2)}) %collective-permute-start.33) | collective-permute-done | bytes 65568 | tf_op jit(solution)/shard_map/ppermute | solution.py:250
  104.1 1.3 %collective-permute-done.34.refs_7_ = bf16[64,512]{1,0:T(8,128)(2,1)S(1)} collective-permute-done((bf16[64,512]{1,0:T(8,128)(2,1)S(1)}, bf16[64,512]{1,0:T(8,128)(2,1)S(1)}, u32[]{:S(2)}, u32[]{:S(2)}) %collective-permute-start.34) | collective-permute-done | bytes 65568 | tf_op jit(solution)/shard_map/ppermute | solution.py:250
  105.4 2.8 %shard_map.42 = bf16[4,512,512]{2,1,0:T(8,128)(2,1)} custom-call(s32[2]{0:T(128)S(1)} %pad_add_fusion.own_ref, f32[4,512]{1,0:T(4,128)S(1)} %copy-done.3, f32[512,512]{1,0:T(8,128)S(1)} %bitcast.7, bf16[528,512]{1,0:T(8,128)(2,1)S(1)} %shard_map.37.head_ref.refs_0_, bf16[3,512,512]{2,1,0:T(8,128)(2,1)S(1)} %get-tuple-element.30.rest_ref, ...), custom_call_target="tpu_custom_call" | custom-call | flops 1073741824 | bytes 3694600 | tf_op jit(solution)/shard_map/pallas_call | solution.py:22
  (63 shorter events, 20.6 us)
Async XLA Ops:
  1.0 12.1 %collective-permute-start = (bf16[128,512]{1,0:T(8,128)(2,1)S(1)}, bf16[128,512]{1,0:T(8,128)(2,1)S(1)}, u32[]{:S(2)}, u32[]{:S(2)}) collective-permute-start(bf16[128,512]{1,0:T(8,128)(2,1)S(1)} %slice_bitcast_fusion.refs_0_), channel_id=1, source_target_pairs={{0,2},{1,3},{2,0},{3,1},{4,6},{5,7},{6,4},{7,5},{8,10},{9,11},{10,... | collective-permute-start | bytes 393224 | tf_op jit(solution)/shard_map/ppermute | solution.py:41
  5.1 8.0 %collective-permute-start.1 = (bf16[128,512]{1,0:T(8,128)(2,1)S(1)}, bf16[128,512]{1,0:T(8,128)(2,1)S(1)}, u32[]{:S(2)}, u32[]{:S(2)}) collective-permute-start(bf16[128,512]{1,0:T(8,128)(2,1)S(1)} %slice_bitcast_fusion.refs_0_), channel_id=1, source_target_pairs={{0,1},{1,0},{2,3},{3,2},{4,5},{5,4},{6,7},{7,6},{8,9},{9,8},{10,11... | collective-permute-start | bytes 393224 | tf_op jit(solution)/shard_map/ppermute | solution.py:41
  6.7 8.7 %collective-permute-start.2 = (bf16[128,512]{1,0:T(8,128)(2,1)S(1)}, bf16[128,512]{1,0:T(8,128)(2,1)S(1)}, u32[]{:S(2)}, u32[]{:S(2)}) collective-permute-start(bf16[128,512]{1,0:T(8,128)(2,1)S(1)} %slice_bitcast_fusion.refs_0_), channel_id=1, source_target_pairs={{0,3},{1,2},{2,1},{3,0},{4,7},{5,6},{6,5},{7,4},{8,11},{9,10},{10,... | collective-permute-start | bytes 393224 | tf_op jit(solution)/shard_map/ppermute | solution.py:41
  16.8 16.6 %collective-permute-start.7 = (bf16[528,512]{1,0:T(8,128)(2,1)S(1)}, bf16[528,512]{1,0:T(8,128)(2,1)S(1)}, u32[]{:S(2)}, u32[]{:S(2)}) collective-permute-start(bf16[528,512]{1,0:T(8,128)(2,1)S(1)} %shard_map.37.head_ref.refs_0_), channel_id=1, source_target_pairs={{0,8},{4,20},{8,0},{12,28},{16,24},{20,4},{24,16},{28,12},{1,9},{5... | collective-permute-start | bytes 1622024 | tf_op jit(solution)/shard_map/ppermute | solution.py:239
  20.2 11.6 %collective-permute-start.15 = (f32[64,512]{1,0:T(8,128)S(1)}, f32[64,512]{1,0:T(8,128)S(1)}, u32[]{:S(2)}, u32[]{:S(2)}) collective-permute-start(f32[64,512]{1,0:T(8,128)S(1)} %get-tuple-element.33), channel_id=1, source_target_pairs={{0,8},{4,12},{8,0},{12,4},{16,24},{20,28},{24,16},{28,20},{1,9},{5... | collective-permute-start | bytes 393224 | tf_op jit(solution)/shard_map/ppermute | solution.py:250
  20.8 13.8 %collective-permute-start.16 = (f32[64,512]{1,0:T(8,128)S(1)}, f32[64,512]{1,0:T(8,128)S(1)}, u32[]{:S(2)}, u32[]{:S(2)}) collective-permute-start(f32[64,512]{1,0:T(8,128)S(1)} %get-tuple-element.34), channel_id=1, source_target_pairs={{0,12},{4,8},{8,4},{12,0},{16,28},{20,24},{24,20},{28,16},{1,13},{... | collective-permute-start | bytes 393224 | tf_op jit(solution)/shard_map/ppermute | solution.py:250
  22.1 16.2 %collective-permute-start.17 = (f32[64,512]{1,0:T(8,128)S(1)}, f32[64,512]{1,0:T(8,128)S(1)}, u32[]{:S(2)}, u32[]{:S(2)}) collective-permute-start(f32[64,512]{1,0:T(8,128)S(1)} %get-tuple-element.35), channel_id=1, source_target_pairs={{0,16},{4,20},{8,24},{12,28},{16,0},{20,4},{24,8},{28,12},{1,17},{... | collective-permute-start | bytes 393224 | tf_op jit(solution)/shard_map/ppermute | solution.py:250
  23.6 19.0 %collective-permute-start.18 = (f32[64,512]{1,0:T(8,128)S(1)}, f32[64,512]{1,0:T(8,128)S(1)}, u32[]{:S(2)}, u32[]{:S(2)}) collective-permute-start(f32[64,512]{1,0:T(8,128)S(1)} %get-tuple-element.36), channel_id=1, source_target_pairs={{0,20},{4,16},{8,28},{12,24},{16,4},{20,0},{24,12},{28,8},{1,21},{... | collective-permute-start | bytes 393224 | tf_op jit(solution)/shard_map/ppermute | solution.py:250
  31.8 31.4 %collective-permute-start.8 = (bf16[528,512]{1,0:T(8,128)(2,1)S(1)}, bf16[528,512]{1,0:T(8,128)(2,1)S(1)}, u32[]{:S(2)}, u32[]{:S(2)}) collective-permute-start(bf16[528,512]{1,0:T(8,128)(2,1)S(1)} %shard_map.37.head_ref.refs_0_), channel_id=1, source_target_pairs={{0,16},{4,12},{8,24},{12,4},{16,0},{20,28},{24,8},{28,20},{1,17},{... | collective-permute-start | bytes 1622024 | tf_op jit(solution)/shard_map/ppermute | solution.py:239
  33.4 30.4 %collective-permute-start.9 = (bf16[528,512]{1,0:T(8,128)(2,1)S(1)}, bf16[528,512]{1,0:T(8,128)(2,1)S(1)}, u32[]{:S(2)}, u32[]{:S(2)}) collective-permute-start(bf16[528,512]{1,0:T(8,128)(2,1)S(1)} %collective-permute-done.7.refs_1_), channel_id=1, source_target_pairs={{0,16},{4,12},{8,24},{12,4},{16,0},{20,28},{24,8},{28,20},{1,17},{... | collective-permute-start | bytes 1622024 | tf_op jit(solution)/shard_map/ppermute | solution.py:239
  34.6 8.0 %collective-permute-start.19 = (f32[64,512]{1,0:T(8,128)S(1)}, f32[64,512]{1,0:T(8,128)S(1)}, u32[]{:S(2)}, u32[]{:S(2)}) collective-permute-start(f32[64,512]{1,0:T(8,128)S(1)} %get-tuple-element.37), channel_id=1, source_target_pairs={{0,24},{4,28},{8,16},{12,20},{16,8},{20,12},{24,0},{28,4},{1,25},{... | collective-permute-start | bytes 393224 | tf_op jit(solution)/shard_map/ppermute | solution.py:250
  38.3 22.6 %collective-permute-start.3 = (bf16[3,128,512]{2,1,0:T(8,128)(2,1)S(1)}, bf16[3,128,512]{2,1,0:T(8,128)(2,1)S(1)}, u32[]{:S(2)}, u32[]{:S(2)}) collective-permute-start(bf16[3,128,512]{2,1,0:T(8,128)(2,1)S(1)} %slice.7.refs_0_), channel_id=1, source_target_pairs={{0,2},{2,0},{1,3},{3,1},{4,6},{6,4},{5,7},{7,5},{8,10},{10,8},{9,1... | collective-permute-start | bytes 1179656 | tf_op jit(solution)/shard_map/ppermute | solution.py:48
  42.6 19.2 %collective-permute-start.4 = (bf16[3,128,512]{2,1,0:T(8,128)(2,1)S(1)}, bf16[3,128,512]{2,1,0:T(8,128)(2,1)S(1)}, u32[]{:S(2)}, u32[]{:S(2)}) collective-permute-start(bf16[3,128,512]{2,1,0:T(8,128)(2,1)S(1)} %slice.7.refs_0_), channel_id=1, source_target_pairs={{0,1},{1,0},{2,3},{3,2},{4,5},{5,4},{6,7},{7,6},{8,9},{9,8},{10,11... | collective-permute-start | bytes 1179656 | tf_op jit(solution)/shard_map/ppermute | solution.py:49
  42.6 20.5 %collective-permute-start.5 = (bf16[3,128,512]{2,1,0:T(8,128)(2,1)S(1)}, bf16[3,128,512]{2,1,0:T(8,128)(2,1)S(1)}, u32[]{:S(2)}, u32[]{:S(2)}) collective-permute-start(bf16[3,128,512]{2,1,0:T(8,128)(2,1)S(1)} %slice.7.refs_0_), channel_id=1, source_target_pairs={{1,2},{2,1},{5,6},{6,5},{9,10},{10,9},{13,14},{14,13},{17,18},{18,... | collective-permute-start | bytes 1179656 | tf_op jit(solution)/shard_map/ppermute | solution.py:50
  60.9 19.1 %collective-permute-start.10 = (bf16[528,512]{1,0:T(8,128)(2,1)S(1)}, bf16[528,512]{1,0:T(8,128)(2,1)S(1)}, u32[]{:S(2)}, u32[]{:S(2)}) collective-permute-start(bf16[528,512]{1,0:T(8,128)(2,1)S(1)} %shard_map.37.head_ref.refs_0_), channel_id=1, source_target_pairs={{0,4},{4,0},{8,12},{12,8},{16,20},{20,16},{24,28},{28,24},{1,5},{5... | collective-permute-start | bytes 1622024 | tf_op jit(solution)/shard_map/ppermute | solution.py:242
  61.8 12.5 %collective-permute-start.6 = (bf16[3,128,512]{2,1,0:T(8,128)(2,1)S(1)}, bf16[3,128,512]{2,1,0:T(8,128)(2,1)S(1)}, u32[]{:S(2)}, u32[]{:S(2)}) collective-permute-start(bf16[3,128,512]{2,1,0:T(8,128)(2,1)S(1)} %collective-permute-done.3.refs_1_), channel_id=1, source_target_pairs={{1,0},{2,3},{5,4},{6,7},{9,8},{10,11},{13,12},{14,15},{17,16},{18,... | collective-permute-start | bytes 1179656 | tf_op jit(solution)/shard_map/ppermute | solution.py:51
  63.1 21.7 %collective-permute-start.11 = (bf16[528,512]{1,0:T(8,128)(2,1)S(1)}, bf16[528,512]{1,0:T(8,128)(2,1)S(1)}, u32[]{:S(2)}, u32[]{:S(2)}) collective-permute-start(bf16[528,512]{1,0:T(8,128)(2,1)S(1)} %collective-permute-done.7.refs_1_), channel_id=1, source_target_pairs={{0,4},{4,0},{8,12},{12,8},{16,20},{20,16},{24,28},{28,24},{1,5},{5... | collective-permute-start | bytes 1622024 | tf_op jit(solution)/shard_map/ppermute | solution.py:242
  63.2 22.3 %collective-permute-start.12 = (bf16[528,512]{1,0:T(8,128)(2,1)S(1)}, bf16[528,512]{1,0:T(8,128)(2,1)S(1)}, u32[]{:S(2)}, u32[]{:S(2)}) collective-permute-start(bf16[528,512]{1,0:T(8,128)(2,1)S(1)} %collective-permute-done.8.refs_2_), channel_id=1, source_target_pairs={{0,4},{4,0},{8,12},{12,8},{16,20},{20,16},{24,28},{28,24},{1,5},{5... | collective-permute-start | bytes 1622024 | tf_op jit(solution)/shard_map/ppermute | solution.py:242
  63.7 22.7 %collective-permute-start.13 = (bf16[528,512]{1,0:T(8,128)(2,1)S(1)}, bf16[528,512]{1,0:T(8,128)(2,1)S(1)}, u32[]{:S(2)}, u32[]{:S(2)}) collective-permute-start(bf16[528,512]{1,0:T(8,128)(2,1)S(1)} %collective-permute-done.9.refs_3_), channel_id=1, source_target_pairs={{0,4},{4,0},{8,12},{12,8},{16,20},{20,16},{24,28},{28,24},{1,5},{5... | collective-permute-start | bytes 1622024 | tf_op jit(solution)/shard_map/ppermute | solution.py:242
  74.4 5.6 %collective-permute-start.20 = (f32[64,512]{1,0:T(8,128)S(1)}, f32[64,512]{1,0:T(8,128)S(1)}, u32[]{:S(2)}, u32[]{:S(2)}) collective-permute-start(f32[64,512]{1,0:T(8,128)S(1)} %get-tuple-element.38), channel_id=1, source_target_pairs={{0,28},{4,24},{8,20},{12,16},{16,12},{20,8},{24,4},{28,0},{1,29},{... | collective-permute-start | bytes 393224 | tf_op jit(solution)/shard_map/ppermute | solution.py:250
  81.2 9.0 %collective-permute-start.23 = (bf16[64,512]{1,0:T(8,128)(2,1)S(1)}, bf16[64,512]{1,0:T(8,128)(2,1)S(1)}, u32[]{:S(2)}, u32[]{:S(2)}) collective-permute-start(bf16[64,512]{1,0:T(8,128)(2,1)S(1)} %get-tuple-element.42), channel_id=1, source_target_pairs={{0,12},{4,8},{8,4},{12,0},{16,28},{20,24},{24,20},{28,16},{1,13},{... | collective-permute-start | bytes 196616 | tf_op jit(solution)/shard_map/ppermute | solution.py:250
  84.8 5.5 %collective-permute-start.24 = (bf16[64,512]{1,0:T(8,128)(2,1)S(1)}, bf16[64,512]{1,0:T(8,128)(2,1)S(1)}, u32[]{:S(2)}, u32[]{:S(2)}) collective-permute-start(bf16[64,512]{1,0:T(8,128)(2,1)S(1)} %get-tuple-element.43), channel_id=1, source_target_pairs={{0,16},{4,20},{8,24},{12,28},{16,0},{20,4},{24,8},{28,12},{1,17},{... | collective-permute-start | bytes 196616 | tf_op jit(solution)/shard_map/ppermute | solution.py:250
  84.8 5.5 %collective-permute-start.25 = (bf16[64,512]{1,0:T(8,128)(2,1)S(1)}, bf16[64,512]{1,0:T(8,128)(2,1)S(1)}, u32[]{:S(2)}, u32[]{:S(2)}) collective-permute-start(bf16[64,512]{1,0:T(8,128)(2,1)S(1)} %get-tuple-element.44), channel_id=1, source_target_pairs={{0,20},{4,16},{8,28},{12,24},{16,4},{20,0},{24,12},{28,8},{1,21},{... | collective-permute-start | bytes 196616 | tf_op jit(solution)/shard_map/ppermute | solution.py:250
  86.4 6.2 %collective-permute-start.27 = (bf16[64,512]{1,0:T(8,128)(2,1)S(1)}, bf16[64,512]{1,0:T(8,128)(2,1)S(1)}, u32[]{:S(2)}, u32[]{:S(2)}) collective-permute-start(bf16[64,512]{1,0:T(8,128)(2,1)S(1)} %get-tuple-element.46), channel_id=1, source_target_pairs={{0,28},{4,24},{8,20},{12,16},{16,12},{20,8},{24,4},{28,0},{1,29},{... | collective-permute-start | bytes 196616 | tf_op jit(solution)/shard_map/ppermute | solution.py:250
  (15 other events, 184.0 us)

commit v2 on v1

--- a/solution.py
+++ b/solution.py
@@ -87,6 +87,8 @@
     depth = bias_ref.shape[0]
     rows, width = guess_ref.shape
     pieces, tau_refs, rest_ref = refs[: -count - 1], refs[-count - 1 : -1], refs[-1]
+    each = len(pieces) // 2
+    early = pieces[0].shape[0]
     rank = own_ref[0]
     part_rows = rows // count
     half = count // 2
@@ -105,7 +107,9 @@
         if layer_no == 0:
             weight = head_ref[pl.ds(0, width), :]
         else:
-            put_pieces(own_ref, [p.at[layer_no - 1] for p in pieces], rest_ref, (layer_no - 1,))
+            at = layer_no - 1
+            here = [p.at[at] for p in pieces[:each]] if at < early else [p.at[at - early] for p in pieces[each:]]
+            put_pieces(own_ref, here, rest_ref, (at,))
             weight = rest_ref[layer_no - 1]
         bias = bias_ref[layer_no : layer_no + 1, :]
         for part in range(2):
@@ -264,7 +268,7 @@
     part = jax.ShapeDtypeStruct((part_rows, width), BF16)
 
     head_pieces = gather_direct(weights[0], "dp")
-    rest_pieces = gather_passed(weights[1:], "dp")
+    rest_pieces = gather_passed(weights[1:-1], "dp") + gather_passed(weights[-1:], "dp")
     guess_parts = call(
         split_kernel,
         (jax.ShapeDtypeStruct((part_rows, width), F32),) * count,

time: 109 us -> 118 us (1.083)
  the two profiles are of different devices: /device:TPU:0 before, /device:TPU:4 now
where the time goes in v2:
time: 118 us; the launch traced here: 116 us
  waiting for transfers between devices  56.8 us (48%)
  starting transfers between devices  47.8 us (41%)
  Pallas kernels  9.71 us (8%)
  local copies, waits for them, and re-layouts  1.8 us (2%)
    ppermute x21, starting transfers between devices, exchange(): lax.ppermute(values[mask], 'layer', [(source, source ^ mask) for source i...  30.4 us
    ppermute x21, waiting for transfers between devices, exchange(): lax.ppermute(values[mask], 'layer', [(source, source ^ mask) for source i...  20.7 us
    ppermute x2, waiting for transfers between devices, gather_passed(): passed = lax.ppermute(across, axis, [(1, 0), (2, 3)])  13 us
    ppermute x2, waiting for transfers between devices, gather_passed(): across = lax.ppermute(piece, axis, [(0, 2), (2, 0), (1, 3), (3, 1)])  12.8 us
    pallas_call x6, Pallas kernels, call(): pl.pallas_call(kernel, out_shape=out_shapes, in_specs=in_specs, out_specs...  9.71 us
    ppermute x3, waiting for transfers between devices, gather_direct(): lax.ppermute(piece, axis, [(source, source ^ mask) for source in range(4)])  8.45 us
    ppermute x3, starting transfers between devices, gather_direct(): lax.ppermute(piece, axis, [(source, source ^ mask) for source in range(4)])  4.45 us
    ppermute x2, starting transfers between devices, gather_passed(): across = lax.ppermute(piece, axis, [(0, 2), (2, 0), (1, 3), (3, 1)])  4.24 us
  transfers between devices with their start and end apart: 39, of which 19 were waited for; matrix products, arithmetic and copies ran while one was open for 0% of the time, Pallas kernels for 3%

profile of v2, /device:TPU:4, one launch (start us, length us, event | category | flops | bytes accessed | tf_op | source)
XLA Modules:
  0.0 116.3 jit_solution(3693669015145838530)
XLA Ops:
  1.1 2.7 %collective-permute-start = (bf16[128,512]{1,0:T(8,128)(2,1)S(1)}, bf16[128,512]{1,0:T(8,128)(2,1)S(1)}, u32[]{:S(2)}, u32[]{:S(2)}) collective-permute-start(bf16[128,512]{1,0:T(8,128)(2,1)S(1)} %get-tuple-element.56.refs_0_), channel_id=1, source_target_pairs={{0,2},{1,3},{2,0},{3,1},{4,6},{5,7},{6,4},{7,5},{8,10},{9,11},{10,... | collective-permute-start | bytes 393224 | tf_op jit(solution)/shard_map/ppermute | solution.py:41
  3.7 1.6 %collective-permute-start.1 = (bf16[128,512]{1,0:T(8,128)(2,1)S(1)}, bf16[128,512]{1,0:T(8,128)(2,1)S(1)}, u32[]{:S(2)}, u32[]{:S(2)}) collective-permute-start(bf16[128,512]{1,0:T(8,128)(2,1)S(1)} %get-tuple-element.56.refs_0_), channel_id=1, source_target_pairs={{0,1},{1,0},{2,3},{3,2},{4,5},{5,4},{6,7},{7,6},{8,9},{9,8},{10,11... | collective-permute-start | bytes 393224 | tf_op jit(solution)/shard_map/ppermute | solution.py:41
  5.6 6.7 %collective-permute-done.refs_1_ = bf16[128,512]{1,0:T(8,128)(2,1)S(1)} collective-permute-done((bf16[128,512]{1,0:T(8,128)(2,1)S(1)}, bf16[128,512]{1,0:T(8,128)(2,1)S(1)}, u32[]{:S(2)}, u32[]{:S(2)}) %collective-permute-start) | collective-permute-done | bytes 131104 | tf_op jit(solution)/shard_map/ppermute | solution.py:41
  12.3 1.8 %collective-permute-done.2.refs_3_ = bf16[128,512]{1,0:T(8,128)(2,1)S(1)} collective-permute-done((bf16[128,512]{1,0:T(8,128)(2,1)S(1)}, bf16[128,512]{1,0:T(8,128)(2,1)S(1)}, u32[]{:S(2)}, u32[]{:S(2)}) %collective-permute-start.2) | collective-permute-done | bytes 131104 | tf_op jit(solution)/shard_map/ppermute | solution.py:41
  16.9 4.2 %collective-permute-start.7 = (bf16[1,128,512]{2,1,0:T(8,128)(2,1)S(1)}, bf16[1,128,512]{2,1,0:T(8,128)(2,1)S(1)}, u32[]{:S(2)}, u32[]{:S(2)}) collective-permute-start(bf16[1,128,512]{2,1,0:T(8,128)(2,1)S(1)} %get-tuple-element.55.refs_5_), channel_id=1, source_target_pairs={{0,2},{2,0},{1,3},{3,1},{4,6},{6,4},{5,7},{7,5},{8,10},{10,8},{9,1... | collective-permute-start | bytes 393224 | tf_op jit(solution)/shard_map/ppermute | solution.py:48
  22.5 4.4 %collective-permute-done.7.refs_6_ = bf16[1,128,512]{2,1,0:T(8,128)(2,1)S(1)} collective-permute-done((bf16[1,128,512]{2,1,0:T(8,128)(2,1)S(1)}, bf16[1,128,512]{2,1,0:T(8,128)(2,1)S(1)}, u32[]{:S(2)}, u32[]{:S(2)}) %collective-permute-start.7) | collective-permute-done | bytes 131104 | tf_op jit(solution)/shard_map/ppermute | solution.py:48
  31.5 3.8 %collective-permute-done.19.refs_2_ = f32[64,512]{1,0:T(8,128)S(1)} collective-permute-done((f32[64,512]{1,0:T(8,128)S(1)}, f32[64,512]{1,0:T(8,128)S(1)}, u32[]{:S(2)}, u32[]{:S(2)}) %collective-permute-start.19) | collective-permute-done | bytes 131104 | tf_op jit(solution)/shard_map/ppermute | solution.py:254
  35.3 10.6 %collective-permute-start.22 = (f32[64,512]{1,0:T(8,128)S(1)}, f32[64,512]{1,0:T(8,128)S(1)}, u32[]{:S(2)}, u32[]{:S(2)}) collective-permute-start(f32[64,512]{1,0:T(8,128)S(1)} %get-tuple-element.36), channel_id=1, source_target_pairs={{0,20},{4,16},{8,28},{12,24},{16,4},{20,0},{24,12},{28,8},{1,21},{... | collective-permute-start | bytes 393224 | tf_op jit(solution)/shard_map/ppermute | solution.py:254
  45.9 2.8 %collective-permute-start.23 = (f32[64,512]{1,0:T(8,128)S(1)}, f32[64,512]{1,0:T(8,128)S(1)}, u32[]{:S(2)}, u32[]{:S(2)}) collective-permute-start(f32[64,512]{1,0:T(8,128)S(1)} %get-tuple-element.37), channel_id=1, source_target_pairs={{0,24},{4,28},{8,16},{12,20},{16,8},{20,12},{24,0},{28,4},{1,25},{... | collective-permute-start | bytes 393224 | tf_op jit(solution)/shard_map/ppermute | solution.py:254
  50.0 2.1 %collective-permute-done.22.refs_5_ = f32[64,512]{1,0:T(8,128)S(1)} collective-permute-done((f32[64,512]{1,0:T(8,128)S(1)}, f32[64,512]{1,0:T(8,128)S(1)}, u32[]{:S(2)}, u32[]{:S(2)}) %collective-permute-start.22) | collective-permute-done | bytes 131104 | tf_op jit(solution)/shard_map/ppermute | solution.py:254
  52.9 3.1 %collective-permute-done.10.refs_9_ = bf16[1,128,512]{2,1,0:T(8,128)(2,1)S(1)} collective-permute-done((bf16[1,128,512]{2,1,0:T(8,128)(2,1)S(1)}, bf16[1,128,512]{2,1,0:T(8,128)(2,1)S(1)}, u32[]{:S(2)}, u32[]{:S(2)}) %collective-permute-start.10) | collective-permute-done | bytes 131104 | tf_op jit(solution)/shard_map/ppermute | solution.py:51
  56.6 8.5 %collective-permute-done.3.refs_1_ = bf16[2,128,512]{2,1,0:T(8,128)(2,1)S(1)} collective-permute-done((bf16[2,128,512]{2,1,0:T(8,128)(2,1)S(1)}, bf16[2,128,512]{2,1,0:T(8,128)(2,1)S(1)}, u32[]{:S(2)}, u32[]{:S(2)}) %collective-permute-start.3) | collective-permute-done | bytes 262176 | tf_op jit(solution)/shard_map/ppermute | solution.py:48
  65.1 1.7 %collective-permute-done.4.refs_2_ = bf16[2,128,512]{2,1,0:T(8,128)(2,1)S(1)} collective-permute-done((bf16[2,128,512]{2,1,0:T(8,128)(2,1)S(1)}, bf16[2,128,512]{2,1,0:T(8,128)(2,1)S(1)}, u32[]{:S(2)}, u32[]{:S(2)}) %collective-permute-start.4) | collective-permute-done | bytes 262176 | tf_op jit(solution)/shard_map/ppermute | solution.py:49
  68.7 9.9 %collective-permute-done.6.refs_4_ = bf16[2,128,512]{2,1,0:T(8,128)(2,1)S(1)} collective-permute-done((bf16[2,128,512]{2,1,0:T(8,128)(2,1)S(1)}, bf16[2,128,512]{2,1,0:T(8,128)(2,1)S(1)}, u32[]{:S(2)}, u32[]{:S(2)}) %collective-permute-start.6) | collective-permute-done | bytes 262176 | tf_op jit(solution)/shard_map/ppermute | solution.py:51
  80.1 2.2 %shard_map.38 = (bf16[64,512]{1,0:T(8,128)(2,1)S(1)}, bf16[64,512]{1,0:T(8,128)(2,1)S(1)}, bf16[64,512]{1,0:T(8,128)(2,1)S(1)}, bf16[64,512]{1,0:T(8,128)(2,1)S(...) custom-call(s32[2]{0:T(128)S(1)} %pad_add_fusion.own_ref, ...), custom_call_target="tpu_custom_call" | custom-call | flops 1073741824 | bytes 3563528 | tf_op jit(solution)/shard_map/pallas_call | solution.py:22
  82.3 3.0 %collective-permute-done.24.refs_7_ = f32[64,512]{1,0:T(8,128)S(1)} collective-permute-done((f32[64,512]{1,0:T(8,128)S(1)}, f32[64,512]{1,0:T(8,128)S(1)}, u32[]{:S(2)}, u32[]{:S(2)}) %collective-permute-start.24) | collective-permute-done | bytes 131104 | tf_op jit(solution)/shard_map/ppermute | solution.py:254
  87.8 3.0 %collective-permute-done.26.refs_10_ = bf16[64,512]{1,0:T(8,128)(2,1)S(1)} collective-permute-done((bf16[64,512]{1,0:T(8,128)(2,1)S(1)}, bf16[64,512]{1,0:T(8,128)(2,1)S(1)}, u32[]{:S(2)}, u32[]{:S(2)}) %collective-permute-start.26) | collective-permute-done | bytes 65568 | tf_op jit(solution)/shard_map/ppermute | solution.py:254
  90.8 2.2 %collective-permute-start.28 = (bf16[64,512]{1,0:T(8,128)(2,1)S(1)}, bf16[64,512]{1,0:T(8,128)(2,1)S(1)}, u32[]{:S(2)}, u32[]{:S(2)}) collective-permute-start(bf16[64,512]{1,0:T(8,128)(2,1)S(1)} %get-tuple-element.43), channel_id=1, source_target_pairs={{0,16},{4,20},{8,24},{12,28},{16,0},{20,4},{24,8},{28,12},{1,17},{... | collective-permute-start | bytes 196616 | tf_op jit(solution)/shard_map/ppermute | solution.py:254
  93.5 2.4 %collective-permute-start.30 = (bf16[64,512]{1,0:T(8,128)(2,1)S(1)}, bf16[64,512]{1,0:T(8,128)(2,1)S(1)}, u32[]{:S(2)}, u32[]{:S(2)}) collective-permute-start(bf16[64,512]{1,0:T(8,128)(2,1)S(1)} %get-tuple-element.45), channel_id=1, source_target_pairs={{0,24},{4,28},{8,16},{12,20},{16,8},{20,12},{24,0},{28,4},{1,25},{... | collective-permute-start | bytes 196616 | tf_op jit(solution)/shard_map/ppermute | solution.py:254
  98.7 1.8 %collective-permute-done.31.refs_15_ = bf16[64,512]{1,0:T(8,128)(2,1)S(1)} collective-permute-done((bf16[64,512]{1,0:T(8,128)(2,1)S(1)}, bf16[64,512]{1,0:T(8,128)(2,1)S(1)}, u32[]{:S(2)}, u32[]{:S(2)}) %collective-permute-start.31) | collective-permute-done | bytes 65568 | tf_op jit(solution)/shard_map/ppermute | solution.py:254
  100.5 2.4 %shard_map.41 = (bf16[64,512]{1,0:T(8,128)(2,1)S(1)}, bf16[64,512]{1,0:T(8,128)(2,1)S(1)}, bf16[64,512]{1,0:T(8,128)(2,1)S(1)}, bf16[64,512]{1,0:T(8,128)(2,1)S(...) custom-call(s32[2]{0:T(128)S(1)} %pad_add_fusion.own_ref, ...), custom_call_target="tpu_custom_call" | custom-call | flops 536870912 | bytes 5898248 | tf_op jit(solution)/shard_map/pallas_call | solution.py:22
  106.6 1.7 %collective-permute-start.37 = (bf16[64,512]{1,0:T(8,128)(2,1)S(1)}, bf16[64,512]{1,0:T(8,128)(2,1)S(1)}, u32[]{:S(2)}, u32[]{:S(2)}) collective-permute-start(bf16[64,512]{1,0:T(8,128)(2,1)S(1)} %get-tuple-element.53), channel_id=1, source_target_pairs={{0,24},{4,28},{8,16},{12,20},{16,8},{20,12},{24,0},{28,4},{1,25},{... | collective-permute-start | bytes 196616 | tf_op jit(solution)/shard_map/ppermute | solution.py:254
  110.3 1.7 %collective-permute-done.37.refs_6_ = bf16[64,512]{1,0:T(8,128)(2,1)S(1)} collective-permute-done((bf16[64,512]{1,0:T(8,128)(2,1)S(1)}, bf16[64,512]{1,0:T(8,128)(2,1)S(1)}, u32[]{:S(2)}, u32[]{:S(2)}) %collective-permute-start.37) | collective-permute-done | bytes 65568 | tf_op jit(solution)/shard_map/ppermute | solution.py:254
  113.5 2.8 %shard_map.42 = bf16[4,512,512]{2,1,0:T(8,128)(2,1)} custom-call(s32[2]{0:T(128)S(1)} %pad_add_fusion.own_ref, f32[4,512]{1,0:T(4,128)S(1)} %copy-done.2, f32[512,512]{1,0:T(8,128)S(1)} %bitcast.7, bf16[528,512]{1,0:T(8,128)(2,1)S(1)} %shard_map.37.head_ref.refs_0_, bf16[3,512,512]{2,1,0:T(8,128)(2,1)S(1)} %get-tuple-element.30.rest_ref, ...), custom_call_target="tpu_custom_call" | custom-call | flops 1073741824 | bytes 3694600 | tf_op jit(solution)/shard_map/pallas_call | solution.py:22
  (71 shorter events, 29.2 us)
Async XLA Ops:
  1.1 11.2 %collective-permute-start = (bf16[128,512]{1,0:T(8,128)(2,1)S(1)}, bf16[128,512]{1,0:T(8,128)(2,1)S(1)}, u32[]{:S(2)}, u32[]{:S(2)}) collective-permute-start(bf16[128,512]{1,0:T(8,128)(2,1)S(1)} %get-tuple-element.56.refs_0_), channel_id=1, source_target_pairs={{0,2},{1,3},{2,0},{3,1},{4,6},{5,7},{6,4},{7,5},{8,10},{9,11},{10,... | collective-permute-start | bytes 393224 | tf_op jit(solution)/shard_map/ppermute | solution.py:41
  3.7 8.6 %collective-permute-start.1 = (bf16[128,512]{1,0:T(8,128)(2,1)S(1)}, bf16[128,512]{1,0:T(8,128)(2,1)S(1)}, u32[]{:S(2)}, u32[]{:S(2)}) collective-permute-start(bf16[128,512]{1,0:T(8,128)(2,1)S(1)} %get-tuple-element.56.refs_0_), channel_id=1, source_target_pairs={{0,1},{1,0},{2,3},{3,2},{4,5},{5,4},{6,7},{7,6},{8,9},{9,8},{10,11... | collective-permute-start | bytes 393224 | tf_op jit(solution)/shard_map/ppermute | solution.py:41
  5.3 8.7 %collective-permute-start.2 = (bf16[128,512]{1,0:T(8,128)(2,1)S(1)}, bf16[128,512]{1,0:T(8,128)(2,1)S(1)}, u32[]{:S(2)}, u32[]{:S(2)}) collective-permute-start(bf16[128,512]{1,0:T(8,128)(2,1)S(1)} %get-tuple-element.56.refs_0_), channel_id=1, source_target_pairs={{0,3},{1,2},{2,1},{3,0},{4,7},{5,6},{6,5},{7,4},{8,11},{9,10},{10,... | collective-permute-start | bytes 393224 | tf_op jit(solution)/shard_map/ppermute | solution.py:41
  15.4 12.8 %collective-permute-start.11 = (bf16[528,512]{1,0:T(8,128)(2,1)S(1)}, bf16[528,512]{1,0:T(8,128)(2,1)S(1)}, u32[]{:S(2)}, u32[]{:S(2)}) collective-permute-start(bf16[528,512]{1,0:T(8,128)(2,1)S(1)} %shard_map.37.head_ref.refs_0_), channel_id=1, source_target_pairs={{0,8},{4,20},{8,0},{12,28},{16,24},{20,4},{24,16},{28,12},{1,9},{5... | collective-permute-start | bytes 1622024 | tf_op jit(solution)/shard_map/ppermute | solution.py:243
  16.9 10.0 %collective-permute-start.7 = (bf16[1,128,512]{2,1,0:T(8,128)(2,1)S(1)}, bf16[1,128,512]{2,1,0:T(8,128)(2,1)S(1)}, u32[]{:S(2)}, u32[]{:S(2)}) collective-permute-start(bf16[1,128,512]{2,1,0:T(8,128)(2,1)S(1)} %get-tuple-element.55.refs_5_), channel_id=1, source_target_pairs={{0,2},{2,0},{1,3},{3,1},{4,6},{6,4},{5,7},{7,5},{8,10},{10,8},{9,1... | collective-permute-start | bytes 393224 | tf_op jit(solution)/shard_map/ppermute | solution.py:48
  21.2 7.8 %collective-permute-start.8 = (bf16[1,128,512]{2,1,0:T(8,128)(2,1)S(1)}, bf16[1,128,512]{2,1,0:T(8,128)(2,1)S(1)}, u32[]{:S(2)}, u32[]{:S(2)}) collective-permute-start(bf16[1,128,512]{2,1,0:T(8,128)(2,1)S(1)} %get-tuple-element.55.refs_5_), channel_id=1, source_target_pairs={{0,1},{1,0},{2,3},{3,2},{4,5},{5,4},{6,7},{7,6},{8,9},{9,8},{10,11... | collective-permute-start | bytes 393224 | tf_op jit(solution)/shard_map/ppermute | solution.py:49
  21.2 9.1 %collective-permute-start.9 = (bf16[1,128,512]{2,1,0:T(8,128)(2,1)S(1)}, bf16[1,128,512]{2,1,0:T(8,128)(2,1)S(1)}, u32[]{:S(2)}, u32[]{:S(2)}) collective-permute-start(bf16[1,128,512]{2,1,0:T(8,128)(2,1)S(1)} %get-tuple-element.55.refs_5_), channel_id=1, source_target_pairs={{1,2},{2,1},{5,6},{6,5},{9,10},{10,9},{13,14},{14,13},{17,18},{18,... | collective-permute-start | bytes 393224 | tf_op jit(solution)/shard_map/ppermute | solution.py:50
  22.5 7.8 %collective-permute-start.18 = (f32[64,512]{1,0:T(8,128)S(1)}, f32[64,512]{1,0:T(8,128)S(1)}, u32[]{:S(2)}, u32[]{:S(2)}) collective-permute-start(f32[64,512]{1,0:T(8,128)S(1)} %get-tuple-element.32), channel_id=1, source_target_pairs={{0,4},{4,0},{8,12},{12,8},{16,20},{20,16},{24,28},{28,24},{1,5},{5... | collective-permute-start | bytes 393224 | tf_op jit(solution)/shard_map/ppermute | solution.py:254
  26.9 39.9 %collective-permute-start.12 = (bf16[528,512]{1,0:T(8,128)(2,1)S(1)}, bf16[528,512]{1,0:T(8,128)(2,1)S(1)}, u32[]{:S(2)}, u32[]{:S(2)}) collective-permute-start(bf16[528,512]{1,0:T(8,128)(2,1)S(1)} %shard_map.37.head_ref.refs_0_), channel_id=1, source_target_pairs={{0,16},{4,12},{8,24},{12,4},{16,0},{20,28},{24,8},{28,20},{1,17},{... | collective-permute-start | bytes 1622024 | tf_op jit(solution)/shard_map/ppermute | solution.py:243
  28.2 39.1 %collective-permute-start.13 = (bf16[528,512]{1,0:T(8,128)(2,1)S(1)}, bf16[528,512]{1,0:T(8,128)(2,1)S(1)}, u32[]{:S(2)}, u32[]{:S(2)}) collective-permute-start(bf16[528,512]{1,0:T(8,128)(2,1)S(1)} %collective-permute-done.11.refs_1_), channel_id=1, source_target_pairs={{0,16},{4,12},{8,24},{12,4},{16,0},{20,28},{24,8},{28,20},{1,17},{... | collective-permute-start | bytes 1622024 | tf_op jit(solution)/shard_map/ppermute | solution.py:243
  28.9 6.4 %collective-permute-start.19 = (f32[64,512]{1,0:T(8,128)S(1)}, f32[64,512]{1,0:T(8,128)S(1)}, u32[]{:S(2)}, u32[]{:S(2)}) collective-permute-start(f32[64,512]{1,0:T(8,128)S(1)} %get-tuple-element.33), channel_id=1, source_target_pairs={{0,8},{4,12},{8,0},{12,4},{16,24},{20,28},{24,16},{28,20},{1,9},{5... | collective-permute-start | bytes 393224 | tf_op jit(solution)/shard_map/ppermute | solution.py:254
  30.2 15.7 %collective-permute-start.20 = (f32[64,512]{1,0:T(8,128)S(1)}, f32[64,512]{1,0:T(8,128)S(1)}, u32[]{:S(2)}, u32[]{:S(2)}) collective-permute-start(f32[64,512]{1,0:T(8,128)S(1)} %get-tuple-element.34), channel_id=1, source_target_pairs={{0,12},{4,8},{8,4},{12,0},{16,28},{20,24},{24,20},{28,16},{1,13},{... | collective-permute-start | bytes 393224 | tf_op jit(solution)/shard_map/ppermute | solution.py:254
  30.2 18.5 %collective-permute-start.21 = (f32[64,512]{1,0:T(8,128)S(1)}, f32[64,512]{1,0:T(8,128)S(1)}, u32[]{:S(2)}, u32[]{:S(2)}) collective-permute-start(f32[64,512]{1,0:T(8,128)S(1)} %get-tuple-element.35), channel_id=1, source_target_pairs={{0,16},{4,20},{8,24},{12,28},{16,0},{20,4},{24,8},{28,12},{1,17},{... | collective-permute-start | bytes 393224 | tf_op jit(solution)/shard_map/ppermute | solution.py:254
  35.3 16.9 %collective-permute-start.22 = (f32[64,512]{1,0:T(8,128)S(1)}, f32[64,512]{1,0:T(8,128)S(1)}, u32[]{:S(2)}, u32[]{:S(2)}) collective-permute-start(f32[64,512]{1,0:T(8,128)S(1)} %get-tuple-element.36), channel_id=1, source_target_pairs={{0,20},{4,16},{8,28},{12,24},{16,4},{20,0},{24,12},{28,8},{1,21},{... | collective-permute-start | bytes 393224 | tf_op jit(solution)/shard_map/ppermute | solution.py:254
  48.7 7.3 %collective-permute-start.10 = (bf16[1,128,512]{2,1,0:T(8,128)(2,1)S(1)}, bf16[1,128,512]{2,1,0:T(8,128)(2,1)S(1)}, u32[]{:S(2)}, u32[]{:S(2)}) collective-permute-start(bf16[1,128,512]{2,1,0:T(8,128)(2,1)S(1)} %collective-permute-done.7.refs_6_), channel_id=1, source_target_pairs={{1,0},{2,3},{5,4},{6,7},{9,8},{10,11},{13,12},{14,15},{17,16},{18,... | collective-permute-start | bytes 393224 | tf_op jit(solution)/shard_map/ppermute | solution.py:51
  52.2 12.9 %collective-permute-start.3 = (bf16[2,128,512]{2,1,0:T(8,128)(2,1)S(1)}, bf16[2,128,512]{2,1,0:T(8,128)(2,1)S(1)}, u32[]{:S(2)}, u32[]{:S(2)}) collective-permute-start(bf16[2,128,512]{2,1,0:T(8,128)(2,1)S(1)} %slice.10.refs_0_), channel_id=1, source_target_pairs={{0,2},{2,0},{1,3},{3,1},{4,6},{6,4},{5,7},{7,5},{8,10},{10,8},{9,1... | collective-permute-start | bytes 786440 | tf_op jit(solution)/shard_map/ppermute | solution.py:48
  52.2 14.6 %collective-permute-start.4 = (bf16[2,128,512]{2,1,0:T(8,128)(2,1)S(1)}, bf16[2,128,512]{2,1,0:T(8,128)(2,1)S(1)}, u32[]{:S(2)}, u32[]{:S(2)}) collective-permute-start(bf16[2,128,512]{2,1,0:T(8,128)(2,1)S(1)} %slice.10.refs_0_), channel_id=1, source_target_pairs={{0,1},{1,0},{2,3},{3,2},{4,5},{5,4},{6,7},{7,6},{8,9},{9,8},{10,11... | collective-permute-start | bytes 786440 | tf_op jit(solution)/shard_map/ppermute | solution.py:49
  56.0 11.4 %collective-permute-start.5 = (bf16[2,128,512]{2,1,0:T(8,128)(2,1)S(1)}, bf16[2,128,512]{2,1,0:T(8,128)(2,1)S(1)}, u32[]{:S(2)}, u32[]{:S(2)}) collective-permute-start(bf16[2,128,512]{2,1,0:T(8,128)(2,1)S(1)} %slice.10.refs_0_), channel_id=1, source_target_pairs={{1,2},{2,1},{5,6},{6,5},{9,10},{10,9},{13,14},{14,13},{17,18},{18,... | collective-permute-start | bytes 786440 | tf_op jit(solution)/shard_map/ppermute | solution.py:50
  65.1 25.7 %collective-permute-start.14 = (bf16[528,512]{1,0:T(8,128)(2,1)S(1)}, bf16[528,512]{1,0:T(8,128)(2,1)S(1)}, u32[]{:S(2)}, u32[]{:S(2)}) collective-permute-start(bf16[528,512]{1,0:T(8,128)(2,1)S(1)} %shard_map.37.head_ref.refs_0_), channel_id=1, source_target_pairs={{0,4},{4,0},{8,12},{12,8},{16,20},{20,16},{24,28},{28,24},{1,5},{5... | collective-permute-start | bytes 1622024 | tf_op jit(solution)/shard_map/ppermute | solution.py:246
  66.8 26.2 %collective-permute-start.15 = (bf16[528,512]{1,0:T(8,128)(2,1)S(1)}, bf16[528,512]{1,0:T(8,128)(2,1)S(1)}, u32[]{:S(2)}, u32[]{:S(2)}) collective-permute-start(bf16[528,512]{1,0:T(8,128)(2,1)S(1)} %collective-permute-done.11.refs_1_), channel_id=1, source_target_pairs={{0,4},{4,0},{8,12},{12,8},{16,20},{20,16},{24,28},{28,24},{1,5},{5... | collective-permute-start | bytes 1622024 | tf_op jit(solution)/shard_map/ppermute | solution.py:246
  66.8 26.7 %collective-permute-start.16 = (bf16[528,512]{1,0:T(8,128)(2,1)S(1)}, bf16[528,512]{1,0:T(8,128)(2,1)S(1)}, u32[]{:S(2)}, u32[]{:S(2)}) collective-permute-start(bf16[528,512]{1,0:T(8,128)(2,1)S(1)} %collective-permute-done.12.refs_2_), channel_id=1, source_target_pairs={{0,4},{4,0},{8,12},{12,8},{16,20},{20,16},{24,28},{28,24},{1,5},{5... | collective-permute-start | bytes 1622024 | tf_op jit(solution)/shard_map/ppermute | solution.py:246
  67.3 28.6 %collective-permute-start.17 = (bf16[528,512]{1,0:T(8,128)(2,1)S(1)}, bf16[528,512]{1,0:T(8,128)(2,1)S(1)}, u32[]{:S(2)}, u32[]{:S(2)}) collective-permute-start(bf16[528,512]{1,0:T(8,128)(2,1)S(1)} %collective-permute-done.13.refs_3_), channel_id=1, source_target_pairs={{0,4},{4,0},{8,12},{12,8},{16,20},{20,16},{24,28},{28,24},{1,5},{5... | collective-permute-start | bytes 1622024 | tf_op jit(solution)/shard_map/ppermute | solution.py:246
  67.4 11.2 %collective-permute-start.6 = (bf16[2,128,512]{2,1,0:T(8,128)(2,1)S(1)}, bf16[2,128,512]{2,1,0:T(8,128)(2,1)S(1)}, u32[]{:S(2)}, u32[]{:S(2)}) collective-permute-start(bf16[2,128,512]{2,1,0:T(8,128)(2,1)S(1)} %collective-permute-done.3.refs_1_), channel_id=1, source_target_pairs={{1,0},{2,3},{5,4},{6,7},{9,8},{10,11},{13,12},{14,15},{17,16},{18,... | collective-permute-start | bytes 786440 | tf_op jit(solution)/shard_map/ppermute | solution.py:51
  78.6 6.6 %collective-permute-start.24 = (f32[64,512]{1,0:T(8,128)S(1)}, f32[64,512]{1,0:T(8,128)S(1)}, u32[]{:S(2)}, u32[]{:S(2)}) collective-permute-start(f32[64,512]{1,0:T(8,128)S(1)} %get-tuple-element.38), channel_id=1, source_target_pairs={{0,28},{4,24},{8,20},{12,16},{16,12},{20,8},{24,4},{28,0},{1,29},{... | collective-permute-start | bytes 393224 | tf_op jit(solution)/shard_map/ppermute | solution.py:254
  (19 other events, 143.6 us)
